TPU v7x, 32 devices: a whole 2x2x4 slice. The times are simulated.
32 devices in a mesh: dp: 4 (over z), group: 8 (over y, x, core).
Axes of the slice: x: 2, y: 2, z: 4, core: 2. Of those that a mesh axis runs over, the one named last changes fastest.
Arguments:
- points: bfloat16 [262144, 1024], P(('dp', 'group')), may hold values from -12 to 12
- block_rows: int32 [2048], P(('dp', 'group')), may hold values from 1 to 128
- block_owner: int32 [2048, 1], P(('dp', 'group')), may hold values from 0 to 31; in each aligned block of 64 rows (0 to 63, 64 to 127, ...) at most 2 rows name the same one
- block_local: int32 [2048], P(('dp', 'group')), may hold values from 0 to 7
- assign_mid: int32 [256, 1], P(('dp', 'group')), may hold values from 0 to 255
- assign_top: int32 [256, 1], P('group'), may hold values from 0 to 255
Outputs:
- level1: float32 [256, 1024], P(('dp', 'group'))
- best: float32 [262144], P(('dp', 'group'))
- level2: float32 [256, 1024], P('group')
- level3: float32 [256, 1024], replicated
Inputs may be any that keep to these rules, and one draw needn't show every extreme that they name: `block_owner`: among the blocks of one device, no owner is named more than 2 times. `assign_mid`: every level-2 cluster is named by at least one level-1 centroid. `assign_top`: every level-3 cluster is named by at least one level-2 centroid.
All inputs are finite; a program needn't handle non-finite values.
Results may differ from a plain program's by a relative error of at most 0.0014.
Values may be sent and summed in bfloat16 or wider, within the bound.
No kernel may reach another device: no remote copies, remote signals or barrier semaphores. Data moves between devices by JAX's collectives and lax.ppermute only.
A program may use at most 64 MiB of HBM per device.

v0:
```python
import jax
import jax.numpy as jnp
from jax import lax
from jax.sharding import PartitionSpec as P

SLOTS = 2
K1_DEV = 8
K2_DEV = 32
K3 = 256


def local(points, block_rows, block_owner, block_local, assign_mid, assign_top):
    highest = lax.Precision.HIGHEST
    device_count = lax.axis_size(("dp", "group"))
    feature_width = points.shape[1]
    point_count = points.shape[0]
    block_count = block_rows.shape[0]
    block_len = point_count // block_count
    position = lax.broadcasted_iota(jnp.int32, (block_count, block_len), 1)
    live_rows = (position < block_rows[:, None]).astype(jnp.bfloat16)
    grouped = points.reshape(block_count, block_len, feature_width)
    block_sums = jnp.einsum("bp,bpd->bd", live_rows, grouped, preferred_element_type=jnp.float32)
    live_count = block_rows.astype(jnp.float32)
    owners = block_owner[:, 0]
    live_column = live_rows.reshape(-1).astype(jnp.float32)
    score_rows = min(point_count, 1024)
    point_blocks = points.reshape(point_count // score_rows, score_rows, feature_width)
    row_index = lax.broadcasted_iota(jnp.int32, (block_count, block_count), 0)
    col_index = lax.broadcasted_iota(jnp.int32, (block_count, block_count), 1)
    earlier = (owners[None, :] == owners[:, None]) & (col_index < row_index)
    slot_rank = jnp.sum(earlier.astype(jnp.int32), axis=1)
    slot_index = owners * SLOTS + slot_rank
    placer = (
        lax.broadcasted_iota(jnp.int32, (device_count * SLOTS, block_count), 0)
        == slot_index[None, :]
    ).astype(jnp.float32)
    send_sums = jnp.dot(placer, block_sums, precision=highest).reshape(
        device_count, SLOTS, feature_width
    )
    send_counts = jnp.dot(placer, live_count, precision=highest).reshape(device_count, SLOTS)
    send_ids = jnp.dot(placer, block_local.astype(jnp.float32), precision=highest).reshape(
        device_count, SLOTS
    )
    got_sums, got_counts, got_ids = (
        lax.all_to_all(send_sums, ("dp", "group"), split_axis=0, concat_axis=0, tiled=True),
        lax.all_to_all(send_counts, ("dp", "group"), split_axis=0, concat_axis=0, tiled=True),
        lax.all_to_all(send_ids, ("dp", "group"), split_axis=0, concat_axis=0, tiled=True),
    )
    local_index = lax.broadcasted_iota(jnp.int32, (K1_DEV, device_count * SLOTS), 0).astype(
        jnp.float32
    )
    picker = (local_index == got_ids.reshape(-1)[None, :]).astype(jnp.float32)
    level1_sums = jnp.dot(
        picker, got_sums.reshape(device_count * SLOTS, feature_width), precision=highest
    )
    level1_counts = jnp.dot(picker, got_counts.reshape(-1), precision=highest)
    level1 = level1_sums / jnp.maximum(level1_counts, 1.0)[:, None]
    rounded = level1.astype(jnp.bfloat16)
    part_rows = lax.all_gather(rounded, ("dp", "group"), axis=0, tiled=True)
    widened = part_rows.astype(jnp.float32)
    half_norm = 0.5 * jnp.sum(widened * widened, axis=1)

    def block_best(values):
        product = lax.dot_general(
            values, part_rows, (((1,), (1,)), ((), ())), preferred_element_type=jnp.float32
        )
        return jnp.max(product - half_norm[None, :], axis=1)

    found = lax.map(block_best, point_blocks).reshape(-1)
    best = found * live_column
    mid_ids = assign_mid[:, 0]
    mid_total = lax.axis_size("group") * K2_DEV
    chooser = (
        lax.broadcasted_iota(jnp.int32, (mid_total, mid_ids.shape[0]), 0) == mid_ids[None, :]
    ).astype(jnp.float32)
    part_sums = jnp.dot(chooser, level1, precision=highest)
    part_counts = jnp.sum(chooser, axis=1)
    all_sums, all_counts = lax.psum((part_sums, part_counts), "dp")
    mid_sums, mid_counts = (
        lax.psum_scatter(all_sums, "group", scatter_dimension=0, tiled=True),
        lax.psum_scatter(all_counts, "group", scatter_dimension=0, tiled=True),
    )
    level2 = mid_sums / mid_counts[:, None]
    top_ids = assign_top[:, 0]
    top_chooser = (
        lax.broadcasted_iota(jnp.int32, (K3, top_ids.shape[0]), 0) == top_ids[None, :]
    ).astype(jnp.float32)
    top_sums = jnp.dot(top_chooser, level2, precision=highest)
    top_counts = jnp.sum(top_chooser, axis=1)
    total_sums, total_counts = lax.psum((top_sums, top_counts), "group")
    level3 = total_sums / total_counts[:, None]
    return (level1, best, level2, level3)


def solution(mesh):
    return jax.shard_map(
        local,
        mesh=mesh,
        in_specs=(
            P(("dp", "group"), None),
            P(("dp", "group")),
            P(("dp", "group"), None),
            P(("dp", "group")),
            P(("dp", "group"), None),
            P("group", None),
        ),
        out_specs=(P(("dp", "group"), None), P(("dp", "group")), P("group", None), P()),
        check_vma=False,
    )
```

profile of v0, /device:TPU:0, one launch (start us, length us, event | category | flops | bytes accessed | tf_op | source)
XLA Modules:
  0.0 218.8 jit_solution(3724974039878984671)
XLA Ops:
  7.2 0.9 convert_reduce_fusion.1
  8.8 0.8 convolution_bitcast_fusion.1
  9.6 0.8 all_to_all.15
  10.3 7.3 %all-to-all-start = ((f32[32,1,2]{2,1,0:T(1,128)}), f32[32,1,2]{2,1,0:T(1,128)S(1)}, u32[]{:S(2)}, u32[]{:S(2)}) async-start(f32[32,1,2]{2,1,0:T(1,128)} %bitcast.5), calls=%async_computation | async-start | bytes 32768 | tf_op jit(solution)/shard_map/all_to_all | solution.py:47
  17.6 0.7 fusion.18
  18.4 8.0 %fusion.14 = f32[64,1,1024]{2,1,0:T(1,128)S(1)} fusion(bf16[64,128,1024]{2,1,0:T(8,128)(2,1)} %bitcast.56, pred[64,128,1]{1,0,2:T(32,128)(4,1)S(1)} %fusion.18), kind=kOutput, calls=%fused_computation.16 | convolution fusion | flops 16777216 | bytes 17047552 | tf_op jit(solution)/shard_map/bp,bpd->bd/dot_general | solution.py:22
  26.6 0.8 all_to_all.18
  27.3 5.8 %all-to-all-start.2 = ((f32[32,1,2]{2,1,0:T(1,128)}), f32[32,1,2]{2,1,0:T(1,128)S(1)}, u32[]{:S(2)}, u32[]{:S(2)}) async-start(f32[32,1,2]{2,1,0:T(1,128)} %bitcast.11), calls=%async_computation.2 | async-start | bytes 32768 | tf_op jit(solution)/shard_map/all_to_all | solution.py:46
  33.4 0.8 reshape.62
  34.3 6.0 %all-to-all-done.2 = f32[32,1,2]{2,1,0:T(1,128)S(1)} async-done(((f32[32,1,2]{2,1,0:T(1,128)}), f32[32,1,2]{2,1,0:T(1,128)S(1)}, u32[]{:S(2)}, u32[]{:S(2)}) %all-to-all-start.2) | async-done | bytes 288 | tf_op jit(solution)/shard_map/all_to_all | solution.py:46
  40.3 2.6 %all-to-all-start.1 = ((f32[32,2,1024]{2,1,0:T(2,128)}), f32[32,2,1024]{2,1,0:T(2,128)S(1)}, u32[]{:S(2)}, u32[]{:S(2)}) async-start(f32[32,2,1024]{2,1,0:T(2,128)} %reshape.62), calls=%async_computation.1 | async-start | bytes 524288 | tf_op jit(solution)/shard_map/all_to_all | solution.py:45
  44.2 0.7 reduce.6
  45.2 8.2 %all-to-all-done.1 = f32[32,2,1024]{2,1,0:T(2,128)S(1)} async-done(((f32[32,2,1024]{2,1,0:T(2,128)}), f32[32,2,1024]{2,1,0:T(2,128)S(1)}, u32[]{:S(2)}, u32[]{:S(2)}) %all-to-all-start.1) | async-done | bytes 262176 | tf_op jit(solution)/shard_map/all_to_all | solution.py:45
  53.9 1.7 fusion.25
  57.0 12.3 %all-reduce.1 = (f32[256]{0:T(256)S(1)}, f32[256]{0:T(256)S(1)}) all-reduce(f32[256]{0:T(256)S(1)} %convert_reduce_fusion.2, f32[256]{0:T(256)S(1)} %convert_reduce_fusion), channel_id=3, replica_groups=mesh['dp'=4,'group'=8] {'group'}, use_global_device_ids=true, to_apply=%region_9.10.clone | all-reduce | flops 512 | bytes 4096
  69.4 9.7 %psum.33 = f32[32]{0:T(128)S(1)} all-reduce(f32[32]{0:T(128)S(1)} %dynamic-slice.1), channel_id=1, replica_groups=mesh['dp'=4,'group'=8] {'dp'}, use_global_device_ids=true, to_apply=%region_8.9 | all-reduce | flops 32 | bytes 256 | tf_op jit(solution)/shard_map/psum | solution.py:78
  79.1 37.8 %all_gather.3 = bf16[256,1024]{1,0:T(8,128)(2,1)S(1)} all-gather(bf16[8,1024]{1,0:T(8,128)(2,1)S(1)} %get-tuple-element.44), channel_id=1, replica_groups=mesh['dp'=4,'group'=8] {'dp','group'}, dimensions={0}, use_global_device_ids=true | all-gather | bytes 540672 | tf_op jit(solution)/shard_map/all_gather | solution.py:59
  117.3 32.5 %all-reduce.7.cloned.1.call-done = f32[32,1024]{1,0:T(8,128)} async-done(((f32[32,1024]{1,0:T(8,128)}), f32[32,1024]{1,0:T(8,128)}) %all-reduce.7.cloned.1.call-update) | async-done | bytes 131088 | tf_op jit(solution)/shard_map/psum | solution.py:78
  149.8 1.0 broadcast_divide_fusion.1
  150.8 1.7 fusion.16
  152.5 20.1 %while.10 = (s32[]{:T(128)}, f32[8,1024]{1,0:T(8,128)S(1)}, bf16[8,1024,1024]{2,1,0:T(8,128)(2,1)}, bf16[256,1024]{1,0:T(8,128)(2,1)S(1)}, f32[256]{0:T(256)S(1)}, /*index=5*/s32[]{:T(128)}, s32[]{:T(128)}) while((s32[]{:T(128)}, f32[8,1024]{1,0:T(8,128)S(1)}, bf16[8,1024,1024]{2,1,0:T(8,128)(2,1)}, bf16[256,1024]{1,0:T(8,128)(2,1)S(1)}, ...), condition=%wide.region_4.5_spmd, body=%wide.region_2.4_spmd.sunk | while | flops 537394176 | bytes 2634845 | solution.py:69
  152.5 2.3 %fusion.45 = f32[1024]{0:T(1024)S(1)} fusion(bf16[256,1024]{1,0:T(8,128)(2,1)S(1)} %get-tuple-element.94, bf16[8,1024,1024]{2,1,0:T(8,128)(2,1)} %get-tuple-element.93, s32[]{:T(128)S(6)} %copy.27, f32[256]{0:T(256)S(1)} %get-tuple-element.95), kind=kOutput, calls=%fused_computation.4.clone.1 | convolution fusion | flops 537394176 | bytes 2626564 | tf_op jit(solution)/shard_map/while/body/eval_jaxpr/dot_general | solution.py:64
  155.0 2.3 %fusion.45 = f32[1024]{0:T(1024)S(1)} fusion(bf16[256,1024]{1,0:T(8,128)(2,1)S(1)} %get-tuple-element.94, bf16[8,1024,1024]{2,1,0:T(8,128)(2,1)} %get-tuple-element.93, s32[]{:T(128)S(6)} %copy.27, f32[256]{0:T(256)S(1)} %get-tuple-element.95), kind=kOutput, calls=%fused_computation.4.clone.1 | convolution fusion | flops 537394176 | bytes 2626564 | tf_op jit(solution)/shard_map/while/body/eval_jaxpr/dot_general | solution.py:64
  157.4 2.5 %fusion.45 = f32[1024]{0:T(1024)S(1)} fusion(bf16[256,1024]{1,0:T(8,128)(2,1)S(1)} %get-tuple-element.94, bf16[8,1024,1024]{2,1,0:T(8,128)(2,1)} %get-tuple-element.93, s32[]{:T(128)S(6)} %copy.27, f32[256]{0:T(256)S(1)} %get-tuple-element.95), kind=kOutput, calls=%fused_computation.4.clone.1 | convolution fusion | flops 537394176 | bytes 2626564 | tf_op jit(solution)/shard_map/while/body/eval_jaxpr/dot_general | solution.py:64
  160.1 2.3 %fusion.45 = f32[1024]{0:T(1024)S(1)} fusion(bf16[256,1024]{1,0:T(8,128)(2,1)S(1)} %get-tuple-element.94, bf16[8,1024,1024]{2,1,0:T(8,128)(2,1)} %get-tuple-element.93, s32[]{:T(128)S(6)} %copy.27, f32[256]{0:T(256)S(1)} %get-tuple-element.95), kind=kOutput, calls=%fused_computation.4.clone.1 | convolution fusion | flops 537394176 | bytes 2626564 | tf_op jit(solution)/shard_map/while/body/eval_jaxpr/dot_general | solution.py:64
  162.6 2.4 %fusion.45 = f32[1024]{0:T(1024)S(1)} fusion(bf16[256,1024]{1,0:T(8,128)(2,1)S(1)} %get-tuple-element.94, bf16[8,1024,1024]{2,1,0:T(8,128)(2,1)} %get-tuple-element.93, s32[]{:T(128)S(6)} %copy.27, f32[256]{0:T(256)S(1)} %get-tuple-element.95), kind=kOutput, calls=%fused_computation.4.clone.1 | convolution fusion | flops 537394176 | bytes 2626564 | tf_op jit(solution)/shard_map/while/body/eval_jaxpr/dot_general | solution.py:64
  165.1 2.4 %fusion.45 = f32[1024]{0:T(1024)S(1)} fusion(bf16[256,1024]{1,0:T(8,128)(2,1)S(1)} %get-tuple-element.94, bf16[8,1024,1024]{2,1,0:T(8,128)(2,1)} %get-tuple-element.93, s32[]{:T(128)S(6)} %copy.27, f32[256]{0:T(256)S(1)} %get-tuple-element.95), kind=kOutput, calls=%fused_computation.4.clone.1 | convolution fusion | flops 537394176 | bytes 2626564 | tf_op jit(solution)/shard_map/while/body/eval_jaxpr/dot_general | solution.py:64
  167.6 2.4 %fusion.45 = f32[1024]{0:T(1024)S(1)} fusion(bf16[256,1024]{1,0:T(8,128)(2,1)S(1)} %get-tuple-element.94, bf16[8,1024,1024]{2,1,0:T(8,128)(2,1)} %get-tuple-element.93, s32[]{:T(128)S(6)} %copy.27, f32[256]{0:T(256)S(1)} %get-tuple-element.95), kind=kOutput, calls=%fused_computation.4.clone.1 | convolution fusion | flops 537394176 | bytes 2626564 | tf_op jit(solution)/shard_map/while/body/eval_jaxpr/dot_general | solution.py:64
  170.1 2.3 %fusion.45 = f32[1024]{0:T(1024)S(1)} fusion(bf16[256,1024]{1,0:T(8,128)(2,1)S(1)} %get-tuple-element.94, bf16[8,1024,1024]{2,1,0:T(8,128)(2,1)} %get-tuple-element.93, s32[]{:T(128)S(6)} %copy.27, f32[256]{0:T(256)S(1)} %get-tuple-element.95), kind=kOutput, calls=%fused_computation.4.clone.1 | convolution fusion | flops 537394176 | bytes 2626564 | tf_op jit(solution)/shard_map/while/body/eval_jaxpr/dot_general | solution.py:64
  172.6 0.7 bitcast_multiply_fusion
  173.3 36.6 %all-reduce.5.cloned.1.call-done = f32[256,1024]{1,0:T(8,128)} async-done(((f32[256,1024]{1,0:T(8,128)}), f32[256,1024]{1,0:T(8,128)}) %all-reduce.5.cloned.1.call-update) | async-done | bytes 1048592 | tf_op jit(solution)/shard_map/psum | solution.py:90
  209.9 2.3 %broadcast_divide_fusion = f32[256,1024]{1,0:T(8,128)} fusion(f32[256,1024]{1,0:T(8,128)} %all-reduce.5.cloned.1.call-done, f32[256]{0:T(256)S(1)} %get-tuple-element.43), kind=kLoop, calls=%fused_computation.12 | loop fusion | flops 262144 | bytes 2098176 | tf_op jit(solution)/shard_map/div | solution.py:91
  (46 shorter events, 5.2 us)
Async XLA Ops:
  7.2 48.5 %copy-start.5 = (u32[32]{0:T(128)S(1)}, u32[32]{0:T(128)}, u32[]{:S(2)}) copy-start(u32[32]{0:T(128)} %constant.25) | copy-start | bytes 388
  7.2 19.3 %copy-start.2 = (s32[64]{0:T(128)S(1)}, s32[64]{0:T(128)}, u32[]{:S(2)}) copy-start(s32[64]{0:T(128)} %param.9) | copy-start | bytes 772
  7.2 46.7 %copy-start.3 = (s32[8,1]{0,1:T(1,128)S(1)}, s32[8,1]{0,1:T(1,128)}, u32[]{:S(2)}) copy-start(s32[8,1]{0,1:T(1,128)} %param.12) | copy-start | bytes 100
  7.2 49.7 %copy-start.4 = (s32[32,1]{0,1:T(1,128)S(1)}, s32[32,1]{0,1:T(1,128)}, u32[]{:S(2)}) copy-start(s32[32,1]{0,1:T(1,128)} %param.13) | copy-start | bytes 388
  10.3 17.0 %all-to-all-start = ((f32[32,1,2]{2,1,0:T(1,128)}), f32[32,1,2]{2,1,0:T(1,128)S(1)}, u32[]{:S(2)}, u32[]{:S(2)}) async-start(f32[32,1,2]{2,1,0:T(1,128)} %bitcast.5), calls=%async_computation | async-start | bytes 32768 | tf_op jit(solution)/shard_map/all_to_all | solution.py:47
  27.3 12.9 %all-to-all-start.2 = ((f32[32,1,2]{2,1,0:T(1,128)}), f32[32,1,2]{2,1,0:T(1,128)S(1)}, u32[]{:S(2)}, u32[]{:S(2)}) async-start(f32[32,1,2]{2,1,0:T(1,128)} %bitcast.11), calls=%async_computation.2 | async-start | bytes 32768 | tf_op jit(solution)/shard_map/all_to_all | solution.py:46
  40.3 13.2 %all-to-all-start.1 = ((f32[32,2,1024]{2,1,0:T(2,128)}), f32[32,2,1024]{2,1,0:T(2,128)S(1)}, u32[]{:S(2)}, u32[]{:S(2)}) async-start(f32[32,2,1024]{2,1,0:T(2,128)} %reshape.62), calls=%async_computation.1 | async-start | bytes 524288 | tf_op jit(solution)/shard_map/all_to_all | solution.py:45
  42.9 74.3 %reduce-scatter.2.cloned.1.call-start = ((), (), s32[]{:S(2)}) async-start(), calls=%async_computation.5 | async-start | bytes 1179648 | tf_op jit(solution)/shard_map/reduce_scatter | solution.py:80
  53.8 98.6 %copy-start.1 = (f32[8,1024]{1,0:T(8,128)}, f32[8,1024]{1,0:T(8,128)S(1)}, u32[]{:S(2)}) copy-start(f32[8,1024]{1,0:T(8,128)S(1)} %get-tuple-element.45) | copy-start | bytes 98308
  55.5 94.2 %all-reduce.7.cloned.1.call-start = ((), (), s32[]{:S(2)}) async-start(), calls=%async_computation.6 | async-start | bytes 262144 | tf_op jit(solution)/shard_map/psum | solution.py:78
  117.2 92.7 %all-reduce.5.cloned.1.call-start = ((), (), s32[]{:S(2)}) async-start(), calls=%async_computation.4 | async-start | bytes 2097152 | tf_op jit(solution)/shard_map/psum | solution.py:90
  150.8 1.7 copy-start
Sparse Core Ops, SparseCore 0:
  55.7 33.9 reduce-scatter.1
  117.3 32.3 all-reduce.6
  153.5 56.3 all-reduce.4
where the time goes:
time: 219 us
  waiting for transfers between devices  83.4 us (38%)
  blocking collectives  59.9 us (27%)
  matrix products  32 us (15%)
  starting transfers between devices  15.9 us (7%)
  between operations  14.6 us (7%)
  other arithmetic  8.07 us (4%)
  local copies, waits for them, and re-layouts  4.82 us (2%)
    all_gather x1, blocking collectives, local(): part_rows = lax.all_gather(rounded, ('dp', 'group'), axis=0, tiled=True)  37.8 us
    psum x1, waiting for transfers between devices, local(): total_sums, total_counts = lax.psum((top_sums, top_counts), 'group')  36.6 us
    psum x1, waiting for transfers between devices, local(): all_sums, all_counts = lax.psum((part_sums, part_counts), 'dp')  32.5 us
    dot_general x8, matrix products, block_best(): lax.dot_general(values, part_rows, (((1,), (1,)), ((), ())), preferred_el...  19 us
    unnamed x1, blocking collectives  12.3 us
    psum x1, blocking collectives, local(): all_sums, all_counts = lax.psum((part_sums, part_counts), 'dp')  9.71 us
    all_to_all x1, waiting for transfers between devices, local(): lax.all_to_all(send_sums, ('dp', 'group'), split_axis=0, concat_axis=0, t...  8.21 us
    dot_general x1, matrix products, local(): jnp.einsum('bp,bpd->bd', live_rows, grouped, preferred_element_type=jnp.f...  8.05 us
  transfers between devices with their start and end apart: 6, of which 4 were waited for; matrix products, arithmetic and copies ran while one was open for 16% of the time, Pallas kernels for 0%

commit v1 on v0

v1 whole, which is shorter than its diff:
```python
import functools

import jax
import jax.numpy as jnp
from jax import lax
from jax.experimental import pallas as pl
from jax.experimental.pallas import tpu as pltpu
from jax.sharding import PartitionSpec as P

SLOTS = 2
K1_DEV = 8
K3 = 256
CHUNK = 32
LANES = 128
TILE = 1024
ALL = ("dp", "group")


def sums_kernel(
    rows_hbm, owner_hbm, local_hbm, points_ref, out_ref, live_ref, parts, rows_ref, owner_ref, local_ref, taken, sems, small,
    *, blocks, block_len
):
    lines, _, width = out_ref.shape
    depth = width - LANES
    pieces = block_len // CHUNK

    def copy(g, n):
        rows = pl.ds(pl.multiple_of(g * block_len, block_len), n * CHUNK)
        return pltpu.make_async_copy(points_ref.at[rows, :], live_ref.at[rows, :], sems.at[g])

    def issue(g, carry):
        n = (rows_ref[g] + CHUNK - 1) // CHUNK
        for c in range(1, pieces + 1):

            @pl.when(n == c)
            def _():
                copy(g, c).start()

        return carry

    scalars = [
        pltpu.make_async_copy(rows_hbm, rows_ref, small.at[0]),
        pltpu.make_async_copy(owner_hbm, owner_ref, small.at[1]),
        pltpu.make_async_copy(local_hbm, local_ref, small.at[2]),
    ]
    for c in scalars:
        c.start()
    scalars[0].wait()
    lax.fori_loop(0, blocks, issue, 0)
    for c in scalars[1:]:
        c.wait()

    def clear(d, carry):
        taken[d] = 0
        return carry

    lax.fori_loop(0, lines // SLOTS, clear, 0)
    if lines > blocks:
        parts[...] = jnp.zeros_like(parts)
    row_index = lax.broadcasted_iota(jnp.int32, (CHUNK, depth), 0)

    def fold(values):
        return jnp.sum(values.astype(jnp.float32).reshape(-1, 8, depth), axis=0)

    def block(g, carry):
        rows = rows_ref[g]
        owner = owner_ref[g]
        slot = taken[owner]
        taken[owner] = slot + 1
        place = pl.multiple_of((owner * SLOTS + slot) * 8, 8)
        n = (rows + CHUNK - 1) // CHUNK
        code = (rows * K1_DEV + local_ref[g]).astype(jnp.float32) * (1.0 / 8)
        parts[depth // LANES, pl.ds(place, 8), :] = jnp.full((8, LANES), code, jnp.float32)
        for c in range(1, pieces + 1):

            @pl.when(n == c)
            def _():
                copy(g, c).wait()
                start = pl.multiple_of(g * block_len, block_len)
                tail = live_ref[pl.ds(start + (c - 1) * CHUNK, CHUNK), :].astype(jnp.float32)
                total = fold(jnp.where(row_index < rows - (c - 1) * CHUNK, tail, 0.0))
                if c > 1:
                    total = total + fold(live_ref[pl.ds(start, (c - 1) * CHUNK), :])
                for j in range(depth // LANES):
                    parts[j, pl.ds(place, 8), :] = total[:, j * LANES : (j + 1) * LANES]

        return carry

    lax.fori_loop(0, blocks, block, 0)
    for i in range(0, lines, 8):
        for j in range(width // LANES):
            lines_of = [parts[j, pl.ds(i * 8 + r, 8, stride=8), :] for r in range(8)]
            while len(lines_of) > 1:
                lines_of = [a + b for a, b in zip(lines_of[::2], lines_of[1::2])]
            out_ref[pl.ds(i, 8), 0, pl.ds(j * LANES, LANES)] = lines_of[0]


def power_of(exponent, bits=7):
    scale = jnp.ones_like(exponent)
    left = exponent
    for b in reversed(range(bits)):
        has = left >= float(1 << b)
        half = float(2.0 ** (1 << b)) if b < bits - 1 else float(2.0**64)
        scale = jnp.where(has, scale * half, scale)
        left = jnp.where(has, left - float(1 << b), left)
    return scale


def level1_kernel(got_ref, mid_ref, top_ref, level1_ref, send_ref, *, parts):
    lines, _, width = got_ref.shape
    depth = width - LANES
    local = lax.broadcasted_iota(jnp.int32, (K1_DEV, LANES), 0).astype(jnp.float32)
    sums = jnp.zeros((K1_DEV, depth), jnp.float32)
    counts = jnp.zeros((K1_DEV, LANES), jnp.float32)
    for i in range(lines):
        line = got_ref[i]
        code = jnp.broadcast_to(line[:, depth:], (K1_DEV, LANES))
        count = jnp.floor(code * (1.0 / K1_DEV))
        mine = (code - count * K1_DEV) == local
        counts = counts + jnp.where(mine, count, 0.0)
        keep = jnp.concatenate([mine] * (depth // LANES), axis=1)
        sums = sums + jnp.where(keep, jnp.broadcast_to(line[:, :depth], (K1_DEV, depth)), 0.0)
    denominator = jnp.concatenate([jnp.maximum(counts, 1.0)] * (depth // LANES), axis=1)
    level1 = sums / denominator
    level1_ref[...] = level1
    top_value = jnp.max(jnp.abs(level1), axis=1, keepdims=True)
    scale = jnp.ones_like(top_value)
    exponent = jnp.zeros_like(top_value)
    for b in (32, 32, 32, 16, 8, 4, 2, 1):
        grown = top_value * scale * float(2.0**b)
        fits = (grown <= 64.0) & (exponent + b <= 100.0)
        scale = jnp.where(fits, scale * float(2.0**b), scale)
        exponent = jnp.where(fits, exponent + b, exponent)
    value = level1 * scale
    split = value * 8193.0
    coarse = split - (split - value)
    rounded = value.astype(jnp.bfloat16).astype(jnp.float32)
    kept = coarse.astype(jnp.bfloat16).astype(jnp.float32) == rounded
    coded = jnp.where(kept, coarse, coarse + (rounded - coarse) * 0.25)
    send_ref[:, pl.ds(0, depth)] = coded
    lane = lax.broadcasted_iota(jnp.int32, (K1_DEV, LANES), 1)
    extra = jnp.where(lane == 0, exponent, 0.0)
    extra = jnp.where(lane == 1, mid_ref[...].astype(jnp.float32), extra)
    for k in range(parts):
        extra = jnp.where(lane == 2 + k, top_ref[:, k : k + 1].astype(jnp.float32), extra)
    send_ref[:, pl.ds(depth, LANES)] = extra


def last_kernel(
    rows_ref, place_ref, points_ref, gathered_ref, best_ref, level2_ref, level3_ref, live_ref, high, low, half_norm, two, three,
    sems, fetched,
    *, origins, group, parts
):
    count, width = gathered_ref.shape
    depth = width - LANES
    second = group * K1_DEV * parts
    block_len = LANES

    def fetch(g, n):
        rows = pl.ds(pl.multiple_of(g * block_len, block_len), n * CHUNK)
        return pltpu.make_async_copy(points_ref.at[rows, :], live_ref.at[rows, :], fetched.at[g])

    def each(g, act):
        n = (rows_ref[g] + CHUNK - 1) // CHUNK
        for c in range(1, block_len // CHUNK + 1):

            @pl.when(n == c)
            def _():
                act(fetch(g, c))

    def issue(g, carry):
        each(g, lambda copy: copy.start())
        return carry

    lax.fori_loop(0, rows_ref.shape[0], issue, 0)
    extra = gathered_ref[:, pl.ds(depth, LANES)]
    value = gathered_ref[:, pl.ds(0, depth)] * (1.0 / power_of(extra[:, 0:1]))
    upper = value.astype(jnp.bfloat16)
    wide = upper.astype(jnp.float32)
    high[...] = upper
    low[...] = (value - wide).astype(jnp.bfloat16)
    half_norm[...] = 0.5 * jnp.sum(wide * wide, axis=1, keepdims=True)

    def total(chooser, upper, lower):
        dims = (((0,), (0,)), ((), ()))
        a = lax.dot_general(chooser, upper, dims, preferred_element_type=jnp.float32)
        b = lax.dot_general(chooser, lower, dims, preferred_element_type=jnp.float32)
        ones = jnp.ones((chooser.shape[0], LANES), jnp.bfloat16)
        n = lax.dot_general(chooser, ones, dims, preferred_element_type=jnp.float32)
        return (a + b) / n[:, 0:1]

    mid = extra[:, 1:2].astype(jnp.int32)
    size = K1_DEV * parts
    owner = (mid // size) ^ place_ref[0]
    inner = mid % size
    index = (inner // K1_DEV) * (group * K1_DEV) + owner * K1_DEV + inner % K1_DEV
    chooser = (index == lax.broadcasted_iota(jnp.int32, (count, second), 1)).astype(jnp.float32).astype(jnp.bfloat16)
    level2 = total(chooser, high[...], low[...])
    for k in range(parts):
        two[pl.ds(k * K1_DEV, K1_DEV), :] = level2[k * group * K1_DEV : k * group * K1_DEV + K1_DEV, :]
    order = [origins.index((0, q)) for q in range(group)]
    tops = [extra[p * K1_DEV : (p + 1) * K1_DEV, 2 + k : 3 + k] for k in range(parts) for p in order]
    top = jnp.concatenate(tops, axis=0).astype(jnp.int32)
    chooser = (top == lax.broadcasted_iota(jnp.int32, (second, K3), 1)).astype(jnp.float32).astype(jnp.bfloat16)
    upper = level2.astype(jnp.bfloat16)
    lower = (level2 - upper.astype(jnp.float32)).astype(jnp.bfloat16)
    three[...] = total(chooser, upper, lower)
    copies = [
        pltpu.make_async_copy(two, level2_ref, sems.at[0]),
        pltpu.make_async_copy(three, level3_ref, sems.at[1]),
    ]
    for c in copies:
        c.start()
    lane = lax.broadcasted_iota(jnp.int32, (1, LANES), 1)

    def scores(t, carry):
        for b in range(TILE // LANES):
            each(t * (TILE // LANES) + b, lambda copy: copy.wait())
        score = lax.dot_general(
            high[...],
            live_ref[pl.ds(pl.multiple_of(t * TILE, TILE), TILE), :],
            (((1,), (1,)), ((), ())),
            preferred_element_type=jnp.float32,
        )
        found = jnp.max(score - half_norm[...], axis=0, keepdims=True)
        for b in range(TILE // LANES):
            g = t * (TILE // LANES) + b
            best_ref[pl.ds(g, 1), :] = jnp.where(lane < rows_ref[g], found[:, b * LANES : (b + 1) * LANES], 0.0)
        return carry

    lax.fori_loop(0, live_ref.shape[0] // TILE, scores, 0)
    for c in copies:
        c.wait()


def gather(values, stages, devices):
    order = [0]
    for masks in stages:
        pieces = [values]
        for m in masks:
            pieces.append(lax.ppermute(values, ALL, [(i, i ^ m) for i in range(devices)]))
        values = jnp.concatenate(pieces, axis=0)
        order = [q ^ m for m in [0] + list(masks) for q in order]
    return values, order


def local(points, block_rows, block_owner, block_local, assign_mid, assign_top):
    dp, group = lax.axis_size("dp"), lax.axis_size("group")
    devices = dp * group
    rows, depth = points.shape
    blocks = block_rows.shape[0]
    parts = assign_top.shape[0] // K1_DEV
    width = depth + LANES
    smem = pl.BlockSpec(memory_space=pltpu.SMEM)
    vmem = pl.BlockSpec(memory_space=pltpu.VMEM)
    hbm = pl.BlockSpec(memory_space=pltpu.HBM)
    sums = pl.pallas_call(
        functools.partial(sums_kernel, blocks=blocks, block_len=rows // blocks),
        out_shape=jax.ShapeDtypeStruct((devices * SLOTS, 1, width), jnp.float32),
        in_specs=[hbm] * 4,
        out_specs=vmem,
        scratch_shapes=[
            pltpu.VMEM((rows, depth), jnp.bfloat16),
            pltpu.VMEM((width // LANES, devices * SLOTS * 8, LANES), jnp.float32),
            pltpu.SMEM((blocks,), jnp.int32),
            pltpu.SMEM((blocks,), jnp.int32),
            pltpu.SMEM((blocks,), jnp.int32),
            pltpu.SMEM((devices,), jnp.int32),
            pltpu.SemaphoreType.DMA((blocks,)),
            pltpu.SemaphoreType.DMA((3,)),
        ],
        compiler_params=pltpu.CompilerParams(vmem_limit_bytes=58 << 20),
        name="block_sums",
    )(block_rows, block_owner[:, 0], block_local, points)
    got = lax.all_to_all(sums, ALL, split_axis=0, concat_axis=0, tiled=True)
    level1, send = pl.pallas_call(
        functools.partial(level1_kernel, parts=parts),
        out_shape=(
            jax.ShapeDtypeStruct((K1_DEV, depth), jnp.float32),
            jax.ShapeDtypeStruct((K1_DEV, width), jnp.float32),
        ),
        in_specs=[vmem] * 3,
        out_specs=(vmem, vmem),
        compiler_params=pltpu.CompilerParams(vmem_limit_bytes=16 << 20),
        name="level1",
    )(got, assign_mid, assign_top.reshape(parts, K1_DEV).T)
    bits = [1 << b for b in reversed(range((devices - 1).bit_length()))]
    gathered, order = gather(send.astype(jnp.float16), [[b] for b in bits], devices)
    origins = [(q // group, q % group) for q in order]
    place = lax.axis_index("group").astype(jnp.int32).reshape(1)
    best, level2, level3 = pl.pallas_call(
        functools.partial(last_kernel, origins=origins, group=group, parts=parts),
        out_shape=(
            jax.ShapeDtypeStruct((blocks, LANES), jnp.float32),
            jax.ShapeDtypeStruct((K1_DEV * parts, depth), jnp.float32),
            jax.ShapeDtypeStruct((K3, depth), jnp.float32),
        ),
        in_specs=[smem, smem, hbm, vmem],
        out_specs=(vmem, pl.BlockSpec(memory_space=pl.ANY), pl.BlockSpec(memory_space=pl.ANY)),
        scratch_shapes=[
            pltpu.VMEM((rows, depth), jnp.bfloat16),
            pltpu.VMEM((devices * K1_DEV, depth), jnp.bfloat16),
            pltpu.VMEM((devices * K1_DEV, depth), jnp.bfloat16),
            pltpu.VMEM((devices * K1_DEV, 1), jnp.float32),
            pltpu.VMEM((K1_DEV * parts, depth), jnp.float32),
            pltpu.VMEM((K3, depth), jnp.float32),
            pltpu.SemaphoreType.DMA((2,)),
            pltpu.SemaphoreType.DMA((blocks,)),
        ],
        compiler_params=pltpu.CompilerParams(vmem_limit_bytes=58 << 20),
        name="scores",
    )(block_rows, place, points, gathered.astype(jnp.float32))
    return (level1, best.reshape(rows), level2, level3)


def solution(mesh):
    return jax.shard_map(
        local,
        mesh=mesh,
        in_specs=(
            P(("dp", "group"), None),
            P(("dp", "group")),
            P(("dp", "group"), None),
            P(("dp", "group")),
            P(("dp", "group"), None),
            P("group", None),
        ),
        out_specs=(P(("dp", "group"), None), P(("dp", "group")), P("group", None), P()),
        check_vma=False,
    )
```

time: 219 us -> 61.2 us (0.28)
  blocking collectives: 59.9 us -> 0 us
  waiting for transfers between devices: 83.4 us -> 27.8 us
  matrix products: 32 us -> 0 us
  Pallas kernels: 0 us -> 20.4 us
  between operations: 14.6 us -> 0.71 us
  starting transfers between devices: 15.9 us -> 9.07 us
  other arithmetic: 8.07 us -> 1.86 us
  local copies, waits for them, and re-layouts: 4.82 us -> 0.93 us
    psum x2 -> x0, waiting for transfers between devices: 69.1 us -> none  [the longest x1 36.6 us: local(): total_sums, total_counts = lax.psum((top_sums, top_counts), 'group')]
    all_gather x1 -> x0, blocking collectives: 37.8 us -> none  [local(): part_rows = lax.all_gather(rounded, ('dp', 'group'), axis=0, tiled=True)]
    dot_general x16 -> x0, matrix products: 32 us -> none  [the longest x8 19 us: block_best(): lax.dot_general(values, part_rows, (((1,), (1,)), ((), ())), preferred_el...]
    pallas_call x0 -> x3, Pallas kernels: none -> 20.4 us  [the longest x1 11.7 us: local(): pl.pallas_call(functools.partial(last_kernel, origins=origins, group=grou...]
    ppermute x0 -> x5, waiting for transfers between devices: none -> 17.8 us  [gather(): lax.ppermute(values, ALL, [(i, i ^ m) for i in range(devices)])]
    unnamed x1 -> x0, blocking collectives: 12.3 us -> none
    psum x1 -> x0, blocking collectives: 9.71 us -> none  [local(): all_sums, all_counts = lax.psum((part_sums, part_counts), 'dp')]
    all_to_all x3 -> x1, starting transfers between devices: 15.7 us -> 7 us  [local(): got = lax.all_to_all(sums, ALL, split_axis=0, concat_axis=0, tiled=True)]
  transfers between devices with their start and end apart: 6 -> 6, of which waited for: 4 -> 6; matrix products, arithmetic and copies ran while one was open for 16% -> 2% of each run, Pallas kernels for 0% -> 0%
where the time goes in v1:
time: 61.2 us; the launch traced here: 60.7 us
  waiting for transfers between devices  27.8 us (45%)
  Pallas kernels  20.4 us (33%)
  starting transfers between devices  9.07 us (15%)
  other arithmetic  1.86 us (3%)
  local copies, waits for them, and re-layouts  0.93 us (2%)
  between operations  0.71 us (1%)
    ppermute x5, waiting for transfers between devices, gather(): lax.ppermute(values, ALL, [(i, i ^ m) for i in range(devices)])  17.8 us
    pallas_call x1, Pallas kernels, local(): pl.pallas_call(functools.partial(last_kernel, origins=origins, group=grou...  11.7 us
    all_to_all x1, waiting for transfers between devices, local(): got = lax.all_to_all(sums, ALL, split_axis=0, concat_axis=0, tiled=True)  9.96 us
    pallas_call x1, Pallas kernels, local(): pl.pallas_call(functools.partial(sums_kernel, blocks=blocks, block_len=ro...  7.92 us
    all_to_all x1, starting transfers between devices, local(): got = lax.all_to_all(sums, ALL, split_axis=0, concat_axis=0, tiled=True)  7 us
    ppermute x5, starting transfers between devices, gather(): lax.ppermute(values, ALL, [(i, i ^ m) for i in range(devices)])  2.07 us
  transfers between devices with their start and end apart: 6, of which 6 were waited for; matrix products, arithmetic and copies ran while one was open for 2% of the time, Pallas kernels for 0%

profile of v1, /device:TPU:0, one launch (start us, length us, event | category | flops | bytes accessed | tf_op | source)
XLA Modules:
  0.0 60.7 jit_solution(17083928287161741314)
XLA Ops:
  0.6 0.0 copy-start.1
  0.6 0.0 copy-start
  0.7 7.9 %block_sums.1 = f32[64,1,1152]{2,1,0:T(1,128)} custom-call(s32[64]{0:T(128)} %rows_ref.1, s32[64]{0:T(128)} %bitcast.6, s32[64]{0:T(128)} %local_hbm.1, bf16[8192,1024]{1,0:T(8,128)(2,1)} %points_ref.3), custom_call_target="tpu_custom_call" | custom-call | tf_op jit(solution)/shard_map/block_sums/pallas_call | solution.py:257
  8.6 7.0 %all-to-all-start = ((f32[64,1,1152]{2,1,0:T(1,128)}), f32[64,1,1152]{2,1,0:T(1,128)S(1)}, u32[]{:S(2)}, u32[]{:S(2)}) async-start(f32[64,1,1152]{2,1,0:T(1,128)} %block_sums.1), calls=%async_computation | async-start | bytes 589824 | tf_op jit(solution)/shard_map/all_to_all | solution.py:275
  15.6 0.5 broadcast.3
  16.1 0.0 copy-done.1
  16.1 0.7 %reduce.3 = s32[32]{0:T(128)S(1)} reduce(s32[32,1]{0,1:T(1,128)S(1)} %copy-done.1, s32[]{:T(128)} %broadcast.3), dimensions={1}, to_apply=%param.11.reduce_sub_computation.3 | reduce | bytes 260 | tf_op args[5]
  16.8 0.1 reshape.17
  16.9 0.1 copy.10
  16.9 0.0 copy-done
  16.9 0.1 copy.11.mid_ref
  17.0 10.0 %all-to-all-done.got_ref = f32[64,1,1152]{2,1,0:T(1,128)S(1)} async-done(((f32[64,1,1152]{2,1,0:T(1,128)}), f32[64,1,1152]{2,1,0:T(1,128)S(1)}, u32[]{:S(2)}, u32[]{:S(2)}) %all-to-all-start) | async-done | bytes 294944 | tf_op jit(solution)/shard_map/all_to_all | solution.py:275
  27.0 0.8 %level1.1 = (f32[8,1024]{1,0:T(8,128)}, f32[8,1152]{1,0:T(8,128)S(1)}) custom-call(f32[64,1,1152]{2,1,0:T(1,128)S(1)} %all-to-all-done.got_ref, s32[8,1]{1,0:T(8,128)S(1)} %copy.11.mid_ref, s32[8,4]{1,0:T(8,128)S(1)} %bitcast.5), custom_call_target="tpu_custom_call" | custom-call | tf_op jit(solution)/shard_map/level1/pallas_call | solution.py:276
  27.8 0.0 collective-permute-start
  27.8 4.6 %collective-permute-done = f16[8,1152]{1,0:T(8,128)(2,1)S(1)} collective-permute-done((f16[8,1152]{1,0:T(8,128)(2,1)S(1)}, f16[8,1152]{1,0:T(8,128)(2,1)S(1)}, u32[]{:S(2)}, u32[]{:S(2)}) %collective-permute-start) | collective-permute-done | bytes 18464 | tf_op jit(solution)/shard_map/ppermute | solution.py:241
  32.5 0.8 %collective-permute-start.1 = (f16[16,1152]{1,0:T(8,128)(2,1)S(1)}, f16[16,1152]{1,0:T(8,128)(2,1)S(1)}, u32[]{:S(2)}, u32[]{:S(2)}) collective-permute-start(f16[16,1152]{1,0:T(8,128)(2,1)S(1)} %pad_maximum_fusion.2), channel_id=1, source_target_pairs={{0,8},{1,9},{2,10},{3,11},{4,12},{5,13},{6,14},{7,15},{8,0},{9,1},... | collective-permute-start | bytes 110600 | tf_op jit(solution)/shard_map/ppermute | solution.py:241
  33.3 3.2 %collective-permute-done.1 = f16[16,1152]{1,0:T(8,128)(2,1)S(1)} collective-permute-done((f16[16,1152]{1,0:T(8,128)(2,1)S(1)}, f16[16,1152]{1,0:T(8,128)(2,1)S(1)}, u32[]{:S(2)}, u32[]{:S(2)}) %collective-permute-start.1) | collective-permute-done | bytes 36896 | tf_op jit(solution)/shard_map/ppermute | solution.py:241
  36.5 0.8 %collective-permute-start.2 = (f16[32,1152]{1,0:T(8,128)(2,1)S(1)}, f16[32,1152]{1,0:T(8,128)(2,1)S(1)}, u32[]{:S(2)}, u32[]{:S(2)}) collective-permute-start(f16[32,1152]{1,0:T(8,128)(2,1)S(1)} %pad_maximum_fusion.1), channel_id=1, source_target_pairs={{0,4},{1,5},{2,6},{3,7},{4,0},{5,1},{6,2},{7,3},{8,12},{9,13},{10,... | collective-permute-start | bytes 221192 | tf_op jit(solution)/shard_map/ppermute | solution.py:241
  37.4 3.6 %collective-permute-done.2 = f16[32,1152]{1,0:T(8,128)(2,1)S(1)} collective-permute-done((f16[32,1152]{1,0:T(8,128)(2,1)S(1)}, f16[32,1152]{1,0:T(8,128)(2,1)S(1)}, u32[]{:S(2)}, u32[]{:S(2)}) %collective-permute-start.2) | collective-permute-done | bytes 73760 | tf_op jit(solution)/shard_map/ppermute | solution.py:241
  41.0 0.4 collective-permute-start.3
  41.4 4.8 %collective-permute-done.3 = f16[64,1152]{1,0:T(8,128)(2,1)S(1)} collective-permute-done((f16[64,1152]{1,0:T(8,128)(2,1)S(1)}, f16[64,1152]{1,0:T(8,128)(2,1)S(1)}, u32[]{:S(2)}, u32[]{:S(2)}) %collective-permute-start.3) | collective-permute-done | bytes 147488 | tf_op jit(solution)/shard_map/ppermute | solution.py:241
  46.3 0.1 collective-permute-start.4
  46.3 1.6 %collective-permute-done.4 = f16[128,1152]{1,0:T(8,128)(2,1)S(1)} collective-permute-done((f16[128,1152]{1,0:T(8,128)(2,1)S(1)}, f16[128,1152]{1,0:T(8,128)(2,1)S(1)}, u32[]{:S(2)}, u32[]{:S(2)}) %collective-permute-start.4) | collective-permute-done | bytes 294944 | tf_op jit(solution)/shard_map/ppermute | solution.py:241
  47.9 0.1 constant_dynamic-update-slice_fusion.5
  48.0 1.1 %convert_element_type.7.gathered_ref = f32[256,1152]{1,0:T(8,128)} convert(f16[256,1152]{1,0:T(8,128)(2,1)S(1)} %constant_dynamic-update-slice_fusion.5) | non-fusion elementwise | flops 294912 | bytes 1769472 | tf_op jit(solution)/shard_map/convert_element_type | solution.py:312
  49.1 11.7 %scores.1 = (f32[64,128]{1,0:T(8,128)}, f32[32,1024]{1,0:T(8,128)}, f32[256,1024]{1,0:T(8,128)}) custom-call(s32[64]{0:T(128)} %rows_ref.1, s32[1]{0:T(128)} %bitcast.2.place_ref, bf16[8192,1024]{1,0:T(8,128)(2,1)} %points_ref.3, f32[256,1152]{1,0:T(8,128)} %convert_element_type.7.gathered_ref), custom_call_target="tpu_custom_call" | custom-call | tf_op jit(solution)/shard_map/scores/pallas_call | solution.py:291
  (9 shorter events, 0.2 us)
Async XLA Ops:
  0.6 15.5 %copy-start.1 = (s32[32,1]{0,1:T(1,128)S(1)}, s32[32,1]{0,1:T(1,128)}, u32[]{:S(2)}) copy-start(s32[32,1]{0,1:T(1,128)} %param.11) | copy-start | bytes 388
  0.6 16.3 %copy-start = (s32[8,1]{0,1:T(1,128)S(1)}, s32[8,1]{0,1:T(1,128)}, u32[]{:S(2)}) copy-start(s32[8,1]{0,1:T(1,128)} %param.10) | copy-start | bytes 100
  8.6 18.4 %all-to-all-start = ((f32[64,1,1152]{2,1,0:T(1,128)}), f32[64,1,1152]{2,1,0:T(1,128)S(1)}, u32[]{:S(2)}, u32[]{:S(2)}) async-start(f32[64,1,1152]{2,1,0:T(1,128)} %block_sums.1), calls=%async_computation | async-start | bytes 589824 | tf_op jit(solution)/shard_map/all_to_all | solution.py:275
  27.8 4.7 %collective-permute-start = (f16[8,1152]{1,0:T(8,128)(2,1)S(1)}, f16[8,1152]{1,0:T(8,128)(2,1)S(1)}, u32[]{:S(2)}, u32[]{:S(2)}) collective-permute-start(f16[8,1152]{1,0:T(8,128)(2,1)S(1)} %get-tuple-element.15), channel_id=1, source_target_pairs={{0,16},{1,17},{2,18},{3,19},{4,20},{5,21},{6,22},{7,23},{8,24},{9,... | collective-permute-start | bytes 55304 | tf_op jit(solution)/shard_map/ppermute | solution.py:241
  32.5 4.0 %collective-permute-start.1 = (f16[16,1152]{1,0:T(8,128)(2,1)S(1)}, f16[16,1152]{1,0:T(8,128)(2,1)S(1)}, u32[]{:S(2)}, u32[]{:S(2)}) collective-permute-start(f16[16,1152]{1,0:T(8,128)(2,1)S(1)} %pad_maximum_fusion.2), channel_id=1, source_target_pairs={{0,8},{1,9},{2,10},{3,11},{4,12},{5,13},{6,14},{7,15},{8,0},{9,1},... | collective-permute-start | bytes 110600 | tf_op jit(solution)/shard_map/ppermute | solution.py:241
  36.5 4.4 %collective-permute-start.2 = (f16[32,1152]{1,0:T(8,128)(2,1)S(1)}, f16[32,1152]{1,0:T(8,128)(2,1)S(1)}, u32[]{:S(2)}, u32[]{:S(2)}) collective-permute-start(f16[32,1152]{1,0:T(8,128)(2,1)S(1)} %pad_maximum_fusion.1), channel_id=1, source_target_pairs={{0,4},{1,5},{2,6},{3,7},{4,0},{5,1},{6,2},{7,3},{8,12},{9,13},{10,... | collective-permute-start | bytes 221192 | tf_op jit(solution)/shard_map/ppermute | solution.py:241
  41.0 5.2 %collective-permute-start.3 = (f16[64,1152]{1,0:T(8,128)(2,1)S(1)}, f16[64,1152]{1,0:T(8,128)(2,1)S(1)}, u32[]{:S(2)}, u32[]{:S(2)}) collective-permute-start(f16[64,1152]{1,0:T(8,128)(2,1)S(1)} %pad_maximum_fusion), channel_id=1, source_target_pairs={{0,2},{1,3},{2,0},{3,1},{4,6},{5,7},{6,4},{7,5},{8,10},{9,11},{10,... | collective-permute-start | bytes 442376 | tf_op jit(solution)/shard_map/ppermute | solution.py:241
  46.3 1.6 %collective-permute-start.4 = (f16[128,1152]{1,0:T(8,128)(2,1)S(1)}, f16[128,1152]{1,0:T(8,128)(2,1)S(1)}, u32[]{:S(2)}, u32[]{:S(2)}) collective-permute-start(f16[128,1152]{1,0:T(8,128)(2,1)S(1)} %get-tuple-element.16), channel_id=1, source_target_pairs={{0,1},{1,0},{2,3},{3,2},{4,5},{5,4},{6,7},{7,6},{8,9},{9,8},{10,11... | collective-permute-start | bytes 884744 | tf_op jit(solution)/shard_map/ppermute | solution.py:241

commit v2 on v1

v2 whole, which is shorter than its diff:
```python
import functools

import jax
import jax.numpy as jnp
from jax import lax
from jax.experimental import pallas as pl
from jax.experimental.pallas import tpu as pltpu
from jax.sharding import PartitionSpec as P

SLOTS = 2
K1_DEV = 8
K3 = 256
CHUNK = 32
LANES = 128
TILE = 2048
ALL = ("dp", "group")


def sums_kernel(rows_hbm, owner_hbm, local_hbm, mid_hbm, top_hbm, points_ref, *refs, blocks, block_len, dp, group, parts):
    out_refs, (ids_ref, live_ref, partial, rows_ref, owner_ref, local_ref, mid_ref, top_ref, taken, sems, small) = (
        refs[:group],
        refs[group:],
    )
    each, width = out_refs[0].shape
    lines = each * group
    depth = width - LANES
    pieces = block_len // CHUNK

    def copy(g, n):
        rows = pl.ds(pl.multiple_of(g * block_len, block_len), n * CHUNK)
        return pltpu.make_async_copy(points_ref.at[rows, :], live_ref.at[rows, :], sems.at[g])

    def issue(g, carry):
        n = (rows_ref[g] + CHUNK - 1) // CHUNK
        for c in range(1, pieces + 1):

            @pl.when(n == c)
            def _():
                copy(g, c).start()

        return carry

    scalars = [
        pltpu.make_async_copy(rows_hbm, rows_ref, small.at[0]),
        pltpu.make_async_copy(owner_hbm, owner_ref, small.at[1]),
        pltpu.make_async_copy(local_hbm, local_ref, small.at[2]),
        pltpu.make_async_copy(mid_hbm, mid_ref, small.at[3]),
        pltpu.make_async_copy(top_hbm, top_ref, small.at[4]),
    ]
    for c in scalars:
        c.start()
    scalars[0].wait()
    lax.fori_loop(0, blocks, issue, 0)
    for c in scalars[1:]:
        c.wait()

    def clear(d, carry):
        taken[d] = 0
        return carry

    lax.fori_loop(0, lines // SLOTS, clear, 0)
    if lines > blocks:
        partial[...] = jnp.zeros_like(partial)
    row_index = lax.broadcasted_iota(jnp.int32, (CHUNK, depth), 0)
    mine, here = lax.axis_index("dp"), lax.axis_index("group")
    sub = lax.broadcasted_iota(jnp.int32, (K1_DEV, LANES), 0)
    lane = lax.broadcasted_iota(jnp.int32, (K1_DEV, LANES), 1)
    ids = jnp.zeros((K1_DEV, LANES), jnp.int32)
    for r in range(K1_DEV):
        ids = jnp.where((sub == r) & (lane == 3), mid_ref[r], ids)
        for p in range(parts):
            ids = jnp.where((sub == r) & (lane == 4 + p), top_ref[p * K1_DEV + r], ids)
    ids_ref[...] = ids.astype(jnp.float32)

    def fold(values):
        return jnp.sum(values.astype(jnp.float32).reshape(-1, 8, depth), axis=0)

    def block(g, carry):
        rows = rows_ref[g]
        owner = owner_ref[g]
        slot = taken[owner]
        taken[owner] = slot + 1
        column = (owner // group) ^ mine
        place = pl.multiple_of(((((owner % group) ^ here) * dp + column) * SLOTS + slot) * 8, 8)
        n = (rows + CHUNK - 1) // CHUNK
        code = (rows * K1_DEV + local_ref[g]).astype(jnp.float32) * (1.0 / 8)
        partial[depth // LANES, pl.ds(place, 8), :] = jnp.full((8, LANES), code, jnp.float32)
        for c in range(1, pieces + 1):

            @pl.when(n == c)
            def _():
                copy(g, c).wait()
                start = pl.multiple_of(g * block_len, block_len)
                tail = live_ref[pl.ds(start + (c - 1) * CHUNK, CHUNK), :].astype(jnp.float32)
                total = fold(jnp.where(row_index < rows - (c - 1) * CHUNK, tail, 0.0))
                if c > 1:
                    total = total + fold(live_ref[pl.ds(start, (c - 1) * CHUNK), :])
                for j in range(depth // LANES):
                    partial[j, pl.ds(place, 8), :] = total[:, j * LANES : (j + 1) * LANES]

        return carry

    lax.fori_loop(0, blocks, block, 0)
    for i in range(0, lines, 8):
        for j in range(width // LANES):
            lines_of = [partial[j, pl.ds(i * 8 + r, 8, stride=8), :] for r in range(8)]
            while len(lines_of) > 1:
                lines_of = [a + b for a, b in zip(lines_of[::2], lines_of[1::2])]
            out_refs[i // each][pl.ds(i % each, 8), pl.ds(j * LANES, LANES)] = lines_of[0]


def power_of(exponent):
    scale = jnp.full_like(exponent, 0.0625)
    left = exponent + 4.0
    for b in (64, 32, 16, 8, 4, 2, 1):
        has = left >= float(b)
        scale = jnp.where(has, scale * float(2.0**b), scale)
        left = jnp.where(has, left - float(b), left)
    return scale


def fitted(values):
    top_value = jnp.max(jnp.abs(values), axis=1, keepdims=True)
    shrink = top_value > 16384.0
    scale = jnp.where(shrink, 0.0625, jnp.ones_like(top_value))
    exponent = jnp.where(shrink, -4.0, jnp.zeros_like(top_value))
    for b in (32, 32, 32, 16, 8, 4, 2, 1):
        fits = (top_value * scale * float(2.0**b) <= 16384.0) & (exponent + b <= 100.0)
        scale = jnp.where(fits, scale * float(2.0**b), scale)
        exponent = jnp.where(fits, exponent + b, exponent)
    value = values * scale
    split = value * 8193.0
    return value, split - (split - value), exponent


def partial_kernel(*refs, dp, group):
    got_refs, (ids_ref, send_ref) = refs[:group], refs[group:]
    width = send_ref.shape[1]
    depth = width - LANES
    local = lax.broadcasted_iota(jnp.int32, (K1_DEV, LANES), 0).astype(jnp.float32)
    lane = lax.broadcasted_iota(jnp.int32, (K1_DEV, LANES), 1)
    for r in range(dp):
        sums = jnp.zeros((K1_DEV, depth), jnp.float32)
        counts = jnp.zeros((K1_DEV, LANES), jnp.float32)
        for g in range(group):
            for t in range(SLOTS):
                line = got_refs[g][pl.ds(r * SLOTS + t, 1), :]
                code = jnp.broadcast_to(line[:, depth:], (K1_DEV, LANES))
                count = jnp.floor(code * (1.0 / K1_DEV))
                mine = (code - count * K1_DEV) == local
                counts = counts + jnp.where(mine, count, 0.0)
                keep = jnp.concatenate([mine] * (depth // LANES), axis=1)
                sums = sums + jnp.where(keep, jnp.broadcast_to(line[:, :depth], (K1_DEV, depth)), 0.0)
        _, coded, exponent = fitted(sums)
        send_ref[pl.ds(r * K1_DEV, K1_DEV), pl.ds(0, depth)] = coded
        many = jnp.floor(counts * (1.0 / 1024))
        extra = ids_ref[...] if r == 0 else jnp.zeros((K1_DEV, LANES), jnp.float32)
        extra = jnp.where(lane == 0, exponent, jnp.where(lane == 1, counts - many * 1024, jnp.where(lane == 2, many, extra)))
        send_ref[pl.ds(r * K1_DEV, K1_DEV), pl.ds(depth, LANES)] = extra


def level1_kernel(*refs, dp, parts):
    pieces, (ids_ref, level1_ref, send_ref) = refs[:dp], refs[dp:]
    width = send_ref.shape[1]
    depth = width - LANES
    lane = lax.broadcasted_iota(jnp.int32, (K1_DEV, LANES), 1)
    for r in range(dp):
        terms, counts = [], []
        for q in range(dp):
            rows = pl.ds((r ^ q) * K1_DEV, K1_DEV)
            extra = pieces[q][rows, pl.ds(depth, LANES)]
            terms.append(pieces[q][rows, pl.ds(0, depth)] * (1.0 / power_of(extra[:, 0:1])))
            counts.append(extra[:, 1:2] + extra[:, 2:3] * 1024.0)
        while len(terms) > 1:
            terms = [a + b for a, b in zip(terms[::2], terms[1::2])]
            counts = [a + b for a, b in zip(counts[::2], counts[1::2])]
        level1 = terms[0] / jnp.maximum(counts[0], 1.0)
        if r == 0:
            level1_ref[...] = level1
        value, coarse, exponent = fitted(level1)
        rounded = value.astype(jnp.bfloat16).astype(jnp.float32)
        kept = coarse.astype(jnp.bfloat16).astype(jnp.float32) == rounded
        coded = jnp.where(kept, coarse, coarse + (rounded - coarse) * 0.25)
        send_ref[pl.ds(r * K1_DEV, K1_DEV), pl.ds(0, depth)] = coded
        mid = pieces[r][pl.ds(0, K1_DEV), pl.ds(depth, LANES)][:, 3:4]
        extra = jnp.where(lane == 0, exponent, jnp.where(lane == 1, mid, 0.0))
        for k in range(parts):
            extra = jnp.where(lane == 2 + k, ids_ref[:, 4 + k : 5 + k], extra)
        send_ref[pl.ds(r * K1_DEV, K1_DEV), pl.ds(depth, LANES)] = extra


def last_kernel(
    rows_ref, live_ref, *refs, origins, group, parts, pieces, tile
):
    gathered, (best_ref, level2_ref, level3_ref, high, low, half_norm, two, three, sems) = refs[:pieces], refs[pieces:]
    size, width = gathered[0].shape
    count = size * pieces
    depth = width - LANES
    second = group * K1_DEV * parts
    extra = jnp.concatenate([ref[:, pl.ds(depth, LANES)] for ref in gathered], axis=0)
    unscale = 1.0 / power_of(extra[:, 0:1])
    for i, ref in enumerate(gathered):
        rows = pl.ds(i * size, size)
        value = ref[:, pl.ds(0, depth)] * unscale[i * size : (i + 1) * size]
        upper = value.astype(jnp.bfloat16)
        wide = upper.astype(jnp.float32)
        high[rows, :] = upper
        low[rows, :] = (value - wide).astype(jnp.bfloat16)
        half_norm[rows, :] = 0.5 * jnp.sum(wide * wide, axis=1, keepdims=True)

    def total(chooser, upper, lower):
        dims = (((0,), (0,)), ((), ()))
        a = lax.dot_general(chooser, upper, dims, preferred_element_type=jnp.float32)
        b = lax.dot_general(chooser, lower, dims, preferred_element_type=jnp.float32)
        ones = jnp.ones((chooser.shape[0], LANES), jnp.bfloat16)
        n = lax.dot_general(chooser, ones, dims, preferred_element_type=jnp.float32)
        return (a + b) / n[:, 0:1]

    mid = extra[:, 1:2].astype(jnp.int32)
    size = K1_DEV * parts
    owner = (mid // size) ^ lax.axis_index("group")
    inner = mid % size
    index = (inner // K1_DEV) * (group * K1_DEV) + owner * K1_DEV + inner % K1_DEV
    chooser = (index == lax.broadcasted_iota(jnp.int32, (count, second), 1)).astype(jnp.float32).astype(jnp.bfloat16)
    level2 = total(chooser, high[...], low[...])
    for k in range(parts):
        two[pl.ds(k * K1_DEV, K1_DEV), :] = level2[k * group * K1_DEV : k * group * K1_DEV + K1_DEV, :]
    order = [origins.index((0, q)) for q in range(group)]
    tops = [extra[p * K1_DEV : (p + 1) * K1_DEV, 2 + k : 3 + k] for k in range(parts) for p in order]
    top = jnp.concatenate(tops, axis=0).astype(jnp.int32)
    chooser = (top == lax.broadcasted_iota(jnp.int32, (second, K3), 1)).astype(jnp.float32).astype(jnp.bfloat16)
    upper = level2.astype(jnp.bfloat16)
    lower = (level2 - upper.astype(jnp.float32)).astype(jnp.bfloat16)
    three[...] = total(chooser, upper, lower)
    copies = [
        pltpu.make_async_copy(two, level2_ref, sems.at[0]),
        pltpu.make_async_copy(three, level3_ref, sems.at[1]),
    ]
    for c in copies:
        c.start()
    lane = lax.broadcasted_iota(jnp.int32, (1, LANES), 1)

    def scores(t, carry):
        score = lax.dot_general(
            high[...],
            live_ref[pl.ds(pl.multiple_of(t * tile, tile), tile), :],
            (((1,), (1,)), ((), ())),
            preferred_element_type=jnp.float32,
        )
        found = jnp.max(score - half_norm[...], axis=0, keepdims=True)
        for b in range(tile // LANES):
            g = t * (tile // LANES) + b
            best_ref[pl.ds(g, 1), :] = jnp.where(lane < rows_ref[g], found[:, b * LANES : (b + 1) * LANES], 0.0)
        return carry

    lax.fori_loop(0, live_ref.shape[0] // tile, scores, 0)
    for c in copies:
        c.wait()


def swap(values, mask, devices):
    return lax.ppermute(values, ALL, [(i, i ^ mask) for i in range(devices)])


def gather(values, group, devices):
    order = [0]
    bit = group
    while bit > 1:
        step = min(4, bit)
        if bit == 8:
            step = 4
        bit //= step
        masks = [bit * q for q in range(1, step)]
        pieces = [values] + [swap(values, m, devices) for m in masks]
        order = [q ^ m for m in [0] + masks for q in order]
        if bit > 1:
            values = jnp.concatenate(pieces, axis=0)
    return pieces, order


def local(points, block_rows, block_owner, block_local, assign_mid, assign_top):
    dp, group = lax.axis_size("dp"), lax.axis_size("group")
    devices = dp * group
    rows, depth = points.shape
    blocks = block_rows.shape[0]
    parts = assign_top.shape[0] // K1_DEV
    width = depth + LANES
    smem = pl.BlockSpec(memory_space=pltpu.SMEM)
    vmem = pl.BlockSpec(memory_space=pltpu.VMEM)
    hbm = pl.BlockSpec(memory_space=pltpu.HBM)
    pieces = pl.pallas_call(
        functools.partial(sums_kernel, blocks=blocks, block_len=rows // blocks, dp=dp, group=group, parts=parts),
        out_shape=tuple(pltpu.VMEM((dp * SLOTS, width), jnp.float32) for _ in range(group))
        + (pltpu.VMEM((K1_DEV, LANES), jnp.float32), pltpu.VMEM((rows, depth), jnp.bfloat16)),
        in_specs=[hbm] * 6,
        out_specs=(vmem,) * (group + 2),
        scratch_shapes=[
            pltpu.VMEM((width // LANES, devices * SLOTS * 8, LANES), jnp.float32),
            pltpu.SMEM((blocks,), jnp.int32),
            pltpu.SMEM((blocks,), jnp.int32),
            pltpu.SMEM((blocks,), jnp.int32),
            pltpu.SMEM((K1_DEV,), jnp.int32),
            pltpu.SMEM((K1_DEV * parts,), jnp.int32),
            pltpu.SMEM((devices,), jnp.int32),
            pltpu.SemaphoreType.DMA((blocks,)),
            pltpu.SemaphoreType.DMA((5,)),
        ],
        compiler_params=pltpu.CompilerParams(vmem_limit_bytes=40 << 20),
        name="block_sums",
    )(block_rows, block_owner[:, 0], block_local, assign_mid[:, 0], assign_top[:, 0], points)
    ids, live = pieces[group:]
    got = [pieces[0]] + [swap(pieces[q], q, devices) for q in range(1, group)]
    own = pl.pallas_call(
        functools.partial(partial_kernel, dp=dp, group=group),
        out_shape=pltpu.VMEM((dp * K1_DEV, width), jnp.float32),
        in_specs=[vmem] * (group + 1),
        out_specs=vmem,
        compiler_params=pltpu.CompilerParams(vmem_limit_bytes=16 << 20),
        name="partial_sums",
    )(*got, ids)
    half = own.astype(jnp.float16)
    others = [swap(half, q * group, devices).astype(jnp.float32) for q in range(1, dp)]
    level1, send = pl.pallas_call(
        functools.partial(level1_kernel, dp=dp, parts=parts),
        out_shape=(
            jax.ShapeDtypeStruct((K1_DEV, depth), jnp.float32),
            pltpu.VMEM((dp * K1_DEV, width), jnp.float32),
        ),
        in_specs=[vmem] * (dp + 1),
        out_specs=(vmem, vmem),
        compiler_params=pltpu.CompilerParams(vmem_limit_bytes=16 << 20),
        name="level1",
    )(own, *others, ids)
    gathered, order = gather(send.astype(jnp.float16), group, devices)
    origins = [(r, q) for q in order for r in range(dp)]
    best, level2, level3 = pl.pallas_call(
        functools.partial(
            last_kernel, origins=origins, group=group, parts=parts, pieces=len(gathered), tile=min(TILE, TILE * K3 // (devices * K1_DEV))
        ),
        out_shape=(
            jax.ShapeDtypeStruct((blocks, LANES), jnp.float32),
            jax.ShapeDtypeStruct((K1_DEV * parts, depth), jnp.float32),
            jax.ShapeDtypeStruct((K3, depth), jnp.float32),
        ),
        in_specs=[smem] + [vmem] * (1 + len(gathered)),
        out_specs=(vmem, pl.BlockSpec(memory_space=pl.ANY), pl.BlockSpec(memory_space=pl.ANY)),
        scratch_shapes=[
            pltpu.VMEM((devices * K1_DEV, depth), jnp.bfloat16),
            pltpu.VMEM((devices * K1_DEV, depth), jnp.bfloat16),
            pltpu.VMEM((devices * K1_DEV, 1), jnp.float32),
            pltpu.VMEM((K1_DEV * parts, depth), jnp.float32),
            pltpu.VMEM((K3, depth), jnp.float32),
            pltpu.SemaphoreType.DMA((2,)),
        ],
        compiler_params=pltpu.CompilerParams(vmem_limit_bytes=40 << 20),
        name="scores",
    )(block_rows, pltpu.with_memory_space_constraint(live, pltpu.VMEM), *[g.astype(jnp.float32) for g in gathered])
    return (level1, best.reshape(rows), level2, level3)


def solution(mesh):
    return jax.shard_map(
        local,
        mesh=mesh,
        in_specs=(
            P(("dp", "group"), None),
            P(("dp", "group")),
            P(("dp", "group"), None),
            P(("dp", "group")),
            P(("dp", "group"), None),
            P("group", None),
        ),
        out_specs=(P(("dp", "group"), None), P(("dp", "group")), P("group", None), P()),
        check_vma=False,
    )
```

time: 61.2 us -> 49.8 us (0.81)
  waiting for transfers between devices: 27.8 us -> 14.3 us
  starting transfers between devices: 9.07 us -> 15.8 us
  Pallas kernels: 20.4 us -> 17 us
  local copies, waits for them, and re-layouts: 0.93 us -> 0 us
    ppermute x5 -> x14, starting transfers between devices: 2.07 us -> 15.8 us  [swap(): return lax.ppermute(values, ALL, [(i, i ^ mask) for i in range(devices)])]
    all_to_all x1 -> x0, waiting for transfers between devices: 9.96 us -> none  [local(): got = lax.all_to_all(sums, ALL, split_axis=0, concat_axis=0, tiled=True)]
    all_to_all x1 -> x0, starting transfers between devices: 7 us -> none  [local(): got = lax.all_to_all(sums, ALL, split_axis=0, concat_axis=0, tiled=True)]
    ppermute x5 -> x14, waiting for transfers between devices: 17.8 us -> 14.3 us  [swap(): return lax.ppermute(values, ALL, [(i, i ^ mask) for i in range(devices)])]
    pallas_call x1, Pallas kernels: 11.7 us -> 8.57 us  [local(): pl.pallas_call(functools.partial(last_kernel, origins=origins, group=grou...]
    concatenate x3 -> x1, other arithmetic: 0.08 us -> 0.92 us  [gather(): values = jnp.concatenate(pieces, axis=0)]
    pallas_call x1, Pallas kernels: 7.92 us -> 7.25 us  [local(): pl.pallas_call(functools.partial(sums_kernel, blocks=blocks, block_len=ro...]
    unnamed x2 -> x0, other arithmetic: 0.67 us -> none
  transfers between devices with their start and end apart: 6 -> 14, of which waited for: 6 -> 9; matrix products, arithmetic and copies ran while one was open for 2% -> 0% of each run, Pallas kernels for 0% -> 0%
where the time goes in v2:
time: 49.8 us; the launch traced here: 49.7 us
  Pallas kernels  17 us (34%)
  starting transfers between devices  15.8 us (32%)
  waiting for transfers between devices  14.3 us (29%)
  other arithmetic  1.84 us (4%)
  between operations  0.69 us (1%)
    ppermute x14, starting transfers between devices, swap(): return lax.ppermute(values, ALL, [(i, i ^ mask) for i in range(devices)])  15.8 us
    ppermute x14, waiting for transfers between devices, swap(): return lax.ppermute(values, ALL, [(i, i ^ mask) for i in range(devices)])  14.3 us
    pallas_call x1, Pallas kernels, local(): pl.pallas_call(functools.partial(last_kernel, origins=origins, group=grou...  8.57 us
    pallas_call x1, Pallas kernels, local(): pl.pallas_call(functools.partial(sums_kernel, blocks=blocks, block_len=ro...  7.25 us
  transfers between devices with their start and end apart: 14, of which 9 were waited for; matrix products, arithmetic and copies ran while one was open for 0% of the time, Pallas kernels for 0%

profile of v2, /device:TPU:0, one launch (start us, length us, event | category | flops | bytes accessed | tf_op | source)
XLA Modules:
  0.0 49.7 jit_solution(695838171984495321)
XLA Ops:
  0.6 7.2 %block_sums.1 = (f32[8,1152]{1,0:T(8,128)S(1)}, f32[8,1152]{1,0:T(8,128)S(1)}, f32[8,1152]{1,0:T(8,128)S(1)}, f32[8,1152]{1,0:T(8,128)S(1)}, f32[8,1152]{1,0:T(8...) custom-call(s32[64]{0:T(128)} %rows_ref.1, ...), custom_call_target="tpu_custom_call" | custom-call | tf_op jit(solution)/shard_map/block_sums/pallas_call | solution.py:291
  7.9 0.7 %collective-permute-start = (f32[8,1152]{1,0:T(8,128)S(1)}, f32[8,1152]{1,0:T(8,128)S(1)}, u32[]{:S(2)}, u32[]{:S(2)}) collective-permute-start(f32[8,1152]{1,0:T(8,128)S(1)} %get-tuple-element.20), channel_id=1, source_target_pairs={{0,1},{1,0},{2,3},{3,2},{4,5},{5,4},{6,7},{7,6},{8,9},{9,8},{10,11... | collective-permute-start | bytes 110600 | tf_op jit(solution)/shard_map/ppermute | solution.py:262
  8.6 2.5 %collective-permute-start.1 = (f32[8,1152]{1,0:T(8,128)S(1)}, f32[8,1152]{1,0:T(8,128)S(1)}, u32[]{:S(2)}, u32[]{:S(2)}) collective-permute-start(f32[8,1152]{1,0:T(8,128)S(1)} %get-tuple-element.21), channel_id=1, source_target_pairs={{0,2},{1,3},{2,0},{3,1},{4,6},{5,7},{6,4},{7,5},{8,10},{9,11},{10,... | collective-permute-start | bytes 110600 | tf_op jit(solution)/shard_map/ppermute | solution.py:262
  11.2 0.0 collective-permute-start.2
  11.2 1.7 %collective-permute-start.3 = (f32[8,1152]{1,0:T(8,128)S(1)}, f32[8,1152]{1,0:T(8,128)S(1)}, u32[]{:S(2)}, u32[]{:S(2)}) collective-permute-start(f32[8,1152]{1,0:T(8,128)S(1)} %get-tuple-element.23), channel_id=1, source_target_pairs={{0,4},{1,5},{2,6},{3,7},{4,0},{5,1},{6,2},{7,3},{8,12},{9,13},{10,... | collective-permute-start | bytes 110600 | tf_op jit(solution)/shard_map/ppermute | solution.py:262
  12.9 2.7 %collective-permute-start.5 = (f32[8,1152]{1,0:T(8,128)S(1)}, f32[8,1152]{1,0:T(8,128)S(1)}, u32[]{:S(2)}, u32[]{:S(2)}) collective-permute-start(f32[8,1152]{1,0:T(8,128)S(1)} %get-tuple-element.25), channel_id=1, source_target_pairs={{0,6},{1,7},{2,4},{3,5},{4,2},{5,3},{6,0},{7,1},{8,14},{9,15},{10,... | collective-permute-start | bytes 110600 | tf_op jit(solution)/shard_map/ppermute | solution.py:262
  15.6 0.0 collective-permute-done.1.refs_2_
  15.6 0.1 collective-permute-start.6
  15.7 0.0 collective-permute-done.2.refs_3_
  15.7 0.0 collective-permute-done.3.refs_4_
  15.7 0.6 %collective-permute-done.4.refs_5_ = f32[8,1152]{1,0:T(8,128)S(1)} collective-permute-done((f32[8,1152]{1,0:T(8,128)S(1)}, f32[8,1152]{1,0:T(8,128)S(1)}, u32[]{:S(2)}, u32[]{:S(2)}) %collective-permute-start.4) | collective-permute-done | bytes 36896 | tf_op jit(solution)/shard_map/ppermute | solution.py:262
  16.4 1.3 %collective-permute-done.5.refs_6_ = f32[8,1152]{1,0:T(8,128)S(1)} collective-permute-done((f32[8,1152]{1,0:T(8,128)S(1)}, f32[8,1152]{1,0:T(8,128)S(1)}, u32[]{:S(2)}, u32[]{:S(2)}) %collective-permute-start.5) | collective-permute-done | bytes 36896 | tf_op jit(solution)/shard_map/ppermute | solution.py:262
  17.7 2.2 %collective-permute-done.6.refs_7_ = f32[8,1152]{1,0:T(8,128)S(1)} collective-permute-done((f32[8,1152]{1,0:T(8,128)S(1)}, f32[8,1152]{1,0:T(8,128)S(1)}, u32[]{:S(2)}, u32[]{:S(2)}) %collective-permute-start.6) | collective-permute-done | bytes 36896 | tf_op jit(solution)/shard_map/ppermute | solution.py:262
  20.0 0.4 partial_sums.1.refs_0_
  20.4 3.5 %collective-permute-start.9 = (f16[32,1152]{1,0:T(8,128)(2,1)S(1)}, f16[32,1152]{1,0:T(8,128)(2,1)S(1)}, u32[]{:S(2)}, u32[]{:S(2)}) collective-permute-start(f16[32,1152]{1,0:T(8,128)(2,1)S(1)} %convert_element_type.21), channel_id=1, source_target_pairs={{0,24},{1,25},{2,26},{3,27},{4,28},{5,29},{6,30},{7,31},{8,16},{9,... | collective-permute-start | bytes 221192 | tf_op jit(solution)/shard_map/ppermute | solution.py:262
  23.9 0.0 collective-permute-start.8
  23.9 0.9 %collective-permute-start.7 = (f16[32,1152]{1,0:T(8,128)(2,1)S(1)}, f16[32,1152]{1,0:T(8,128)(2,1)S(1)}, u32[]{:S(2)}, u32[]{:S(2)}) collective-permute-start(f16[32,1152]{1,0:T(8,128)(2,1)S(1)} %convert_element_type.21), channel_id=1, source_target_pairs={{0,8},{1,9},{2,10},{3,11},{4,12},{5,13},{6,14},{7,15},{8,0},{9,1},... | collective-permute-start | bytes 221192 | tf_op jit(solution)/shard_map/ppermute | solution.py:262
  24.8 2.3 %collective-permute-done.9 = f16[32,1152]{1,0:T(8,128)(2,1)S(1)} collective-permute-done((f16[32,1152]{1,0:T(8,128)(2,1)S(1)}, f16[32,1152]{1,0:T(8,128)(2,1)S(1)}, u32[]{:S(2)}, u32[]{:S(2)}) %collective-permute-start.9) | collective-permute-done | bytes 73760 | tf_op jit(solution)/shard_map/ppermute | solution.py:262
  27.1 3.4 %collective-permute-done.8 = f16[32,1152]{1,0:T(8,128)(2,1)S(1)} collective-permute-done((f16[32,1152]{1,0:T(8,128)(2,1)S(1)}, f16[32,1152]{1,0:T(8,128)(2,1)S(1)}, u32[]{:S(2)}, u32[]{:S(2)}) %collective-permute-start.8) | collective-permute-done | bytes 73760 | tf_op jit(solution)/shard_map/ppermute | solution.py:262
  30.5 0.0 collective-permute-done.7
  30.6 0.8 %level1.1 = (f32[8,1024]{1,0:T(8,128)}, f32[32,1152]{1,0:T(8,128)S(1)}) custom-call(f32[32,1152]{1,0:T(8,128)S(1)} %partial_sums.1.refs_0_, f32[32,1152]{1,0:T(8,128)S(1)} %convert_element_type.22.refs_1_, f32[32,1152]{1,0:T(8,128)S(1)} %convert_element_type.23.refs_2_, f32[32,1152]{1,0:T(8,128)S(1)} %convert_element_type.24.refs_3_, ...), custom_call_target="tpu_custom_call" | custom-call | tf_op jit(solution)/shard_map/level1/pallas_call | solution.py:323
  31.4 1.1 %collective-permute-start.12 = (f16[32,1152]{1,0:T(8,128)(2,1)S(1)}, f16[32,1152]{1,0:T(8,128)(2,1)S(1)}, u32[]{:S(2)}, u32[]{:S(2)}) collective-permute-start(f16[32,1152]{1,0:T(8,128)(2,1)S(1)} %convert_element_type.25), channel_id=1, source_target_pairs={{0,6},{1,7},{2,4},{3,5},{4,2},{5,3},{6,0},{7,1},{8,14},{9,15},{10,... | collective-permute-start | bytes 221192 | tf_op jit(solution)/shard_map/ppermute | solution.py:262
  32.5 0.9 %collective-permute-start.11 = (f16[32,1152]{1,0:T(8,128)(2,1)S(1)}, f16[32,1152]{1,0:T(8,128)(2,1)S(1)}, u32[]{:S(2)}, u32[]{:S(2)}) collective-permute-start(f16[32,1152]{1,0:T(8,128)(2,1)S(1)} %convert_element_type.25), channel_id=1, source_target_pairs={{0,4},{1,5},{2,6},{3,7},{4,0},{5,1},{6,2},{7,3},{8,12},{9,13},{10,... | collective-permute-start | bytes 221192 | tf_op jit(solution)/shard_map/ppermute | solution.py:262
  33.4 1.5 %collective-permute-start.10 = (f16[32,1152]{1,0:T(8,128)(2,1)S(1)}, f16[32,1152]{1,0:T(8,128)(2,1)S(1)}, u32[]{:S(2)}, u32[]{:S(2)}) collective-permute-start(f16[32,1152]{1,0:T(8,128)(2,1)S(1)} %convert_element_type.25), channel_id=1, source_target_pairs={{0,2},{1,3},{2,0},{3,1},{4,6},{5,7},{6,4},{7,5},{8,10},{9,11},{10,... | collective-permute-start | bytes 221192 | tf_op jit(solution)/shard_map/ppermute | solution.py:262
  34.9 2.2 %collective-permute-done.12 = f16[32,1152]{1,0:T(8,128)(2,1)S(1)} collective-permute-done((f16[32,1152]{1,0:T(8,128)(2,1)S(1)}, f16[32,1152]{1,0:T(8,128)(2,1)S(1)}, u32[]{:S(2)}, u32[]{:S(2)}) %collective-permute-start.12) | collective-permute-done | bytes 73760 | tf_op jit(solution)/shard_map/ppermute | solution.py:262
  37.1 0.5 collective-permute-done.11
  37.5 0.2 collective-permute-done.10
  37.7 0.9 %pad_maximum_fusion = (f16[128,1152]{1,0:T(8,128)(2,1)S(1)}, f32[128,1152]{1,0:T(8,128)}) fusion(f16[32,1152]{1,0:T(8,128)(2,1)S(1)} %collective-permute-done.12, f16[32,1152]{1,0:T(8,128)(2,1)S(1)} %collective-permute-done.11, f16[32,1152]{1,0:T(8,128)(2,1)S(1)} %collective-permute-done.10, f16[32,1152]{1,0:T(8,128)(2,1)S(1)} %convert_element_type.25), kind=kLoop, calls=%fused_computation | loop fusion | flops 589824 | bytes 1179648 | tf_op jit(solution)/shard_map/concatenate | solution.py:277
  38.6 0.0 collective-permute-start.13
  38.6 1.6 %collective-permute-done.13 = f16[128,1152]{1,0:T(8,128)(2,1)S(1)} collective-permute-done((f16[128,1152]{1,0:T(8,128)(2,1)S(1)}, f16[128,1152]{1,0:T(8,128)(2,1)S(1)}, u32[]{:S(2)}, u32[]{:S(2)}) %collective-permute-start.13) | collective-permute-done | bytes 294944 | tf_op jit(solution)/shard_map/ppermute | solution.py:262
  40.2 0.9 %convert_element_type.27.refs_1_ = f32[128,1152]{1,0:T(8,128)} convert(f16[128,1152]{1,0:T(8,128)(2,1)S(1)} %collective-permute-done.13) | non-fusion elementwise | flops 147456 | bytes 884736 | tf_op jit(solution)/shard_map/convert_element_type | solution.py:357
  41.1 8.6 %scores.1 = (f32[64,128]{1,0:T(8,128)}, f32[32,1024]{1,0:T(8,128)}, f32[256,1024]{1,0:T(8,128)}) custom-call(s32[64]{0:T(128)} %rows_ref.1, bf16[8192,1024]{1,0:T(8,128)(2,1)S(1)} %get-tuple-element.29.live_ref, f32[128,1152]{1,0:T(8,128)} %get-tuple-element.35.refs_0_, f32[128,1152]{1,0:T(8,128)} %convert_element_type.27.refs_1_), custom_call_target="tpu_custom_call" | custom-call | tf_op jit(solution)/shard_map/scores/pallas_call | solution.py:336
  (7 shorter events, 0.1 us)
Async XLA Ops:
  7.9 5.0 %collective-permute-start = (f32[8,1152]{1,0:T(8,128)S(1)}, f32[8,1152]{1,0:T(8,128)S(1)}, u32[]{:S(2)}, u32[]{:S(2)}) collective-permute-start(f32[8,1152]{1,0:T(8,128)S(1)} %get-tuple-element.20), channel_id=1, source_target_pairs={{0,1},{1,0},{2,3},{3,2},{4,5},{5,4},{6,7},{7,6},{8,9},{9,8},{10,11... | collective-permute-start | bytes 110600 | tf_op jit(solution)/shard_map/ppermute | solution.py:262
  8.6 7.0 %collective-permute-start.1 = (f32[8,1152]{1,0:T(8,128)S(1)}, f32[8,1152]{1,0:T(8,128)S(1)}, u32[]{:S(2)}, u32[]{:S(2)}) collective-permute-start(f32[8,1152]{1,0:T(8,128)S(1)} %get-tuple-element.21), channel_id=1, source_target_pairs={{0,2},{1,3},{2,0},{3,1},{4,6},{5,7},{6,4},{7,5},{8,10},{9,11},{10,... | collective-permute-start | bytes 110600 | tf_op jit(solution)/shard_map/ppermute | solution.py:262
  11.2 4.6 %collective-permute-start.2 = (f32[8,1152]{1,0:T(8,128)S(1)}, f32[8,1152]{1,0:T(8,128)S(1)}, u32[]{:S(2)}, u32[]{:S(2)}) collective-permute-start(f32[8,1152]{1,0:T(8,128)S(1)} %get-tuple-element.22), channel_id=1, source_target_pairs={{0,3},{1,2},{2,1},{3,0},{4,7},{5,6},{6,5},{7,4},{8,11},{9,10},{10,... | collective-permute-start | bytes 110600 | tf_op jit(solution)/shard_map/ppermute | solution.py:262
  11.2 4.6 %collective-permute-start.3 = (f32[8,1152]{1,0:T(8,128)S(1)}, f32[8,1152]{1,0:T(8,128)S(1)}, u32[]{:S(2)}, u32[]{:S(2)}) collective-permute-start(f32[8,1152]{1,0:T(8,128)S(1)} %get-tuple-element.23), channel_id=1, source_target_pairs={{0,4},{1,5},{2,6},{3,7},{4,0},{5,1},{6,2},{7,3},{8,12},{9,13},{10,... | collective-permute-start | bytes 110600 | tf_op jit(solution)/shard_map/ppermute | solution.py:262
  12.9 3.5 %collective-permute-start.4 = (f32[8,1152]{1,0:T(8,128)S(1)}, f32[8,1152]{1,0:T(8,128)S(1)}, u32[]{:S(2)}, u32[]{:S(2)}) collective-permute-start(f32[8,1152]{1,0:T(8,128)S(1)} %get-tuple-element.24), channel_id=1, source_target_pairs={{0,5},{1,4},{2,7},{3,6},{4,1},{5,0},{6,3},{7,2},{8,13},{9,12},{10,... | collective-permute-start | bytes 110600 | tf_op jit(solution)/shard_map/ppermute | solution.py:262
  12.9 4.9 %collective-permute-start.5 = (f32[8,1152]{1,0:T(8,128)S(1)}, f32[8,1152]{1,0:T(8,128)S(1)}, u32[]{:S(2)}, u32[]{:S(2)}) collective-permute-start(f32[8,1152]{1,0:T(8,128)S(1)} %get-tuple-element.25), channel_id=1, source_target_pairs={{0,6},{1,7},{2,4},{3,5},{4,2},{5,3},{6,0},{7,1},{8,14},{9,15},{10,... | collective-permute-start | bytes 110600 | tf_op jit(solution)/shard_map/ppermute | solution.py:262
  15.6 4.3 %collective-permute-start.6 = (f32[8,1152]{1,0:T(8,128)S(1)}, f32[8,1152]{1,0:T(8,128)S(1)}, u32[]{:S(2)}, u32[]{:S(2)}) collective-permute-start(f32[8,1152]{1,0:T(8,128)S(1)} %get-tuple-element.26), channel_id=1, source_target_pairs={{0,7},{1,6},{2,5},{3,4},{4,3},{5,2},{6,1},{7,0},{8,15},{9,14},{10,... | collective-permute-start | bytes 110600 | tf_op jit(solution)/shard_map/ppermute | solution.py:262
  20.4 6.7 %collective-permute-start.9 = (f16[32,1152]{1,0:T(8,128)(2,1)S(1)}, f16[32,1152]{1,0:T(8,128)(2,1)S(1)}, u32[]{:S(2)}, u32[]{:S(2)}) collective-permute-start(f16[32,1152]{1,0:T(8,128)(2,1)S(1)} %convert_element_type.21), channel_id=1, source_target_pairs={{0,24},{1,25},{2,26},{3,27},{4,28},{5,29},{6,30},{7,31},{8,16},{9,... | collective-permute-start | bytes 221192 | tf_op jit(solution)/shard_map/ppermute | solution.py:262
  23.9 6.6 %collective-permute-start.8 = (f16[32,1152]{1,0:T(8,128)(2,1)S(1)}, f16[32,1152]{1,0:T(8,128)(2,1)S(1)}, u32[]{:S(2)}, u32[]{:S(2)}) collective-permute-start(f16[32,1152]{1,0:T(8,128)(2,1)S(1)} %convert_element_type.21), channel_id=1, source_target_pairs={{0,16},{1,17},{2,18},{3,19},{4,20},{5,21},{6,22},{7,23},{8,24},{9,... | collective-permute-start | bytes 221192 | tf_op jit(solution)/shard_map/ppermute | solution.py:262
  23.9 6.6 %collective-permute-start.7 = (f16[32,1152]{1,0:T(8,128)(2,1)S(1)}, f16[32,1152]{1,0:T(8,128)(2,1)S(1)}, u32[]{:S(2)}, u32[]{:S(2)}) collective-permute-start(f16[32,1152]{1,0:T(8,128)(2,1)S(1)} %convert_element_type.21), channel_id=1, source_target_pairs={{0,8},{1,9},{2,10},{3,11},{4,12},{5,13},{6,14},{7,15},{8,0},{9,1},... | collective-permute-start | bytes 221192 | tf_op jit(solution)/shard_map/ppermute | solution.py:262
  31.4 5.7 %collective-permute-start.12 = (f16[32,1152]{1,0:T(8,128)(2,1)S(1)}, f16[32,1152]{1,0:T(8,128)(2,1)S(1)}, u32[]{:S(2)}, u32[]{:S(2)}) collective-permute-start(f16[32,1152]{1,0:T(8,128)(2,1)S(1)} %convert_element_type.25), channel_id=1, source_target_pairs={{0,6},{1,7},{2,4},{3,5},{4,2},{5,3},{6,0},{7,1},{8,14},{9,15},{10,... | collective-permute-start | bytes 221192 | tf_op jit(solution)/shard_map/ppermute | solution.py:262
  32.5 5.1 %collective-permute-start.11 = (f16[32,1152]{1,0:T(8,128)(2,1)S(1)}, f16[32,1152]{1,0:T(8,128)(2,1)S(1)}, u32[]{:S(2)}, u32[]{:S(2)}) collective-permute-start(f16[32,1152]{1,0:T(8,128)(2,1)S(1)} %convert_element_type.25), channel_id=1, source_target_pairs={{0,4},{1,5},{2,6},{3,7},{4,0},{5,1},{6,2},{7,3},{8,12},{9,13},{10,... | collective-permute-start | bytes 221192 | tf_op jit(solution)/shard_map/ppermute | solution.py:262
  33.4 4.4 %collective-permute-start.10 = (f16[32,1152]{1,0:T(8,128)(2,1)S(1)}, f16[32,1152]{1,0:T(8,128)(2,1)S(1)}, u32[]{:S(2)}, u32[]{:S(2)}) collective-permute-start(f16[32,1152]{1,0:T(8,128)(2,1)S(1)} %convert_element_type.25), channel_id=1, source_target_pairs={{0,2},{1,3},{2,0},{3,1},{4,6},{5,7},{6,4},{7,5},{8,10},{9,11},{10,... | collective-permute-start | bytes 221192 | tf_op jit(solution)/shard_map/ppermute | solution.py:262
  38.6 1.6 %collective-permute-start.13 = (f16[128,1152]{1,0:T(8,128)(2,1)S(1)}, f16[128,1152]{1,0:T(8,128)(2,1)S(1)}, u32[]{:S(2)}, u32[]{:S(2)}) collective-permute-start(f16[128,1152]{1,0:T(8,128)(2,1)S(1)} %get-tuple-element.34), channel_id=1, source_target_pairs={{0,1},{1,0},{2,3},{3,2},{4,5},{5,4},{6,7},{7,6},{8,9},{9,8},{10,11... | collective-permute-start | bytes 884744 | tf_op jit(solution)/shard_map/ppermute | solution.py:262

commit v3 on v2

--- a/solution.py
+++ b/solution.py
@@ -12,7 +12,7 @@
 K3 = 256
 CHUNK = 32
 LANES = 128
-TILE = 2048
+TILE = 4096
 ALL = ("dp", "group")
 
 
@@ -214,7 +214,7 @@
         b = lax.dot_general(chooser, lower, dims, preferred_element_type=jnp.float32)
         ones = jnp.ones((chooser.shape[0], LANES), jnp.bfloat16)
         n = lax.dot_general(chooser, ones, dims, preferred_element_type=jnp.float32)
-        return (a + b) / n[:, 0:1]
+        return (a + b) * jnp.concatenate([1.0 / n] * (depth // LANES), axis=1)
 
     mid = extra[:, 1:2].astype(jnp.int32)
     size = K1_DEV * parts
@@ -263,18 +263,13 @@
 
 
 def gather(values, group, devices):
-    order = [0]
-    bit = group
+    pieces, order, bit = [values], [0], group
     while bit > 1:
         step = min(4, bit)
-        if bit == 8:
-            step = 4
         bit //= step
         masks = [bit * q for q in range(1, step)]
-        pieces = [values] + [swap(values, m, devices) for m in masks]
+        pieces = pieces + [swap(p, m, devices) for m in masks for p in pieces]
         order = [q ^ m for m in [0] + masks for q in order]
-        if bit > 1:
-            values = jnp.concatenate(pieces, axis=0)
     return pieces, order
 
 
@@ -332,6 +327,8 @@
         name="level1",
     )(own, *others, ids)
     gathered, order = gather(send.astype(jnp.float16), group, devices)
+    near = len(gathered) // 2
+    gathered = [jnp.concatenate(gathered[:near], axis=0), jnp.concatenate(gathered[near:], axis=0)]
     origins = [(r, q) for q in order for r in range(dp)]
     best, level2, level3 = pl.pallas_call(
         functools.partial(

time: 49.8 us -> 48.1 us (0.966)
  waiting for transfers between devices: 14.3 us -> 12.7 us
  Pallas kernels: 17 us -> 16.5 us
  starting transfers between devices: 15.8 us -> 16.3 us
    ppermute x14 -> x17, waiting for transfers between devices: 14.3 us -> 12.7 us  [swap(): return lax.ppermute(values, ALL, [(i, i ^ mask) for i in range(devices)])]
    convert_element_type x1 -> x2, other arithmetic: 0.86 us -> 1.78 us  [local(): g.astype(jnp.float32)]
    concatenate x1 -> x0, other arithmetic: 0.92 us -> none  [gather(): values = jnp.concatenate(pieces, axis=0)]
    ppermute x14 -> x17, starting transfers between devices: 15.8 us -> 16.3 us  [swap(): return lax.ppermute(values, ALL, [(i, i ^ mask) for i in range(devices)])]
  transfers between devices with their start and end apart: 14 -> 17, of which waited for: 9 -> 7; matrix products, arithmetic and copies ran while one was open for 0% -> 2% of each run, Pallas kernels for 0% -> 0%
where the time goes in v3:
time: 48.1 us; the launch traced here: 48 us
  Pallas kernels  16.5 us (34%)
  starting transfers between devices  16.3 us (34%)
  waiting for transfers between devices  12.7 us (26%)
  other arithmetic  1.84 us (4%)
  between operations  0.7 us (1%)
    ppermute x17, starting transfers between devices, swap(): return lax.ppermute(values, ALL, [(i, i ^ mask) for i in range(devices)])  16.3 us
    ppermute x17, waiting for transfers between devices, swap(): return lax.ppermute(values, ALL, [(i, i ^ mask) for i in range(devices)])  12.7 us
    pallas_call x1, Pallas kernels, local(): pl.pallas_call(functools.partial(last_kernel, origins=origins, group=grou...  8.11 us
    pallas_call x1, Pallas kernels, local(): pl.pallas_call(functools.partial(sums_kernel, blocks=blocks, block_len=ro...  7.22 us
    convert_element_type x2, other arithmetic, local(): g.astype(jnp.float32)  1.78 us
  transfers between devices with their start and end apart: 17, of which 7 were waited for; matrix products, arithmetic and copies ran while one was open for 2% of the time, Pallas kernels for 0%

profile of v3, /device:TPU:0, one launch (start us, length us, event | category | flops | bytes accessed | tf_op | source)
XLA Modules:
  0.0 48.0 jit_solution(17636328359998326859)
XLA Ops:
  0.6 7.2 %block_sums.1 = (f32[8,1152]{1,0:T(8,128)S(1)}, f32[8,1152]{1,0:T(8,128)S(1)}, f32[8,1152]{1,0:T(8,128)S(1)}, f32[8,1152]{1,0:T(8,128)S(1)}, f32[8,1152]{1,0:T(8...) custom-call(s32[64]{0:T(128)} %rows_ref.1, ...), custom_call_target="tpu_custom_call" | custom-call | tf_op jit(solution)/shard_map/block_sums/pallas_call | solution.py:286
  7.9 0.6 %collective-permute-start = (f32[8,1152]{1,0:T(8,128)S(1)}, f32[8,1152]{1,0:T(8,128)S(1)}, u32[]{:S(2)}, u32[]{:S(2)}) collective-permute-start(f32[8,1152]{1,0:T(8,128)S(1)} %get-tuple-element.20), channel_id=1, source_target_pairs={{0,1},{1,0},{2,3},{3,2},{4,5},{5,4},{6,7},{7,6},{8,9},{9,8},{10,11... | collective-permute-start | bytes 110600 | tf_op jit(solution)/shard_map/ppermute | solution.py:262
  8.4 2.5 %collective-permute-start.1 = (f32[8,1152]{1,0:T(8,128)S(1)}, f32[8,1152]{1,0:T(8,128)S(1)}, u32[]{:S(2)}, u32[]{:S(2)}) collective-permute-start(f32[8,1152]{1,0:T(8,128)S(1)} %get-tuple-element.21), channel_id=1, source_target_pairs={{0,2},{1,3},{2,0},{3,1},{4,6},{5,7},{6,4},{7,5},{8,10},{9,11},{10,... | collective-permute-start | bytes 110600 | tf_op jit(solution)/shard_map/ppermute | solution.py:262
  10.9 0.0 collective-permute-start.2
  11.0 1.9 %collective-permute-start.3 = (f32[8,1152]{1,0:T(8,128)S(1)}, f32[8,1152]{1,0:T(8,128)S(1)}, u32[]{:S(2)}, u32[]{:S(2)}) collective-permute-start(f32[8,1152]{1,0:T(8,128)S(1)} %get-tuple-element.23), channel_id=1, source_target_pairs={{0,4},{1,5},{2,6},{3,7},{4,0},{5,1},{6,2},{7,3},{8,12},{9,13},{10,... | collective-permute-start | bytes 110600 | tf_op jit(solution)/shard_map/ppermute | solution.py:262
  12.9 0.0 collective-permute-start.4
  12.9 0.0 collective-permute-done.refs_1_
  12.9 2.6 %collective-permute-start.5 = (f32[8,1152]{1,0:T(8,128)S(1)}, f32[8,1152]{1,0:T(8,128)S(1)}, u32[]{:S(2)}, u32[]{:S(2)}) collective-permute-start(f32[8,1152]{1,0:T(8,128)S(1)} %get-tuple-element.25), channel_id=1, source_target_pairs={{0,6},{1,7},{2,4},{3,5},{4,2},{5,3},{6,0},{7,1},{8,14},{9,15},{10,... | collective-permute-start | bytes 110600 | tf_op jit(solution)/shard_map/ppermute | solution.py:262
  15.5 0.1 collective-permute-start.6
  15.6 0.8 %collective-permute-done.4.refs_5_ = f32[8,1152]{1,0:T(8,128)S(1)} collective-permute-done((f32[8,1152]{1,0:T(8,128)S(1)}, f32[8,1152]{1,0:T(8,128)S(1)}, u32[]{:S(2)}, u32[]{:S(2)}) %collective-permute-start.4) | collective-permute-done | bytes 36896 | tf_op jit(solution)/shard_map/ppermute | solution.py:262
  16.4 1.3 %collective-permute-done.5.refs_6_ = f32[8,1152]{1,0:T(8,128)S(1)} collective-permute-done((f32[8,1152]{1,0:T(8,128)S(1)}, f32[8,1152]{1,0:T(8,128)S(1)}, u32[]{:S(2)}, u32[]{:S(2)}) %collective-permute-start.5) | collective-permute-done | bytes 36896 | tf_op jit(solution)/shard_map/ppermute | solution.py:262
  17.7 2.1 %collective-permute-done.6.refs_7_ = f32[8,1152]{1,0:T(8,128)S(1)} collective-permute-done((f32[8,1152]{1,0:T(8,128)S(1)}, f32[8,1152]{1,0:T(8,128)S(1)}, u32[]{:S(2)}, u32[]{:S(2)}) %collective-permute-start.6) | collective-permute-done | bytes 36896 | tf_op jit(solution)/shard_map/ppermute | solution.py:262
  19.8 0.4 partial_sums.1.refs_0_
  20.2 3.8 %collective-permute-start.9 = (f16[32,1152]{1,0:T(8,128)(2,1)S(1)}, f16[32,1152]{1,0:T(8,128)(2,1)S(1)}, u32[]{:S(2)}, u32[]{:S(2)}) collective-permute-start(f16[32,1152]{1,0:T(8,128)(2,1)S(1)} %convert_element_type.21), channel_id=1, source_target_pairs={{0,24},{1,25},{2,26},{3,27},{4,28},{5,29},{6,30},{7,31},{8,16},{9,... | collective-permute-start | bytes 221192 | tf_op jit(solution)/shard_map/ppermute | solution.py:262
  24.1 0.6 %collective-permute-start.7 = (f16[32,1152]{1,0:T(8,128)(2,1)S(1)}, f16[32,1152]{1,0:T(8,128)(2,1)S(1)}, u32[]{:S(2)}, u32[]{:S(2)}) collective-permute-start(f16[32,1152]{1,0:T(8,128)(2,1)S(1)} %convert_element_type.21), channel_id=1, source_target_pairs={{0,8},{1,9},{2,10},{3,11},{4,12},{5,13},{6,14},{7,15},{8,0},{9,1},... | collective-permute-start | bytes 221192 | tf_op jit(solution)/shard_map/ppermute | solution.py:262
  24.7 2.4 %collective-permute-done.9 = f16[32,1152]{1,0:T(8,128)(2,1)S(1)} collective-permute-done((f16[32,1152]{1,0:T(8,128)(2,1)S(1)}, f16[32,1152]{1,0:T(8,128)(2,1)S(1)}, u32[]{:S(2)}, u32[]{:S(2)}) %collective-permute-start.9) | collective-permute-done | bytes 73760 | tf_op jit(solution)/shard_map/ppermute | solution.py:262
  27.1 3.4 %collective-permute-done.8 = f16[32,1152]{1,0:T(8,128)(2,1)S(1)} collective-permute-done((f16[32,1152]{1,0:T(8,128)(2,1)S(1)}, f16[32,1152]{1,0:T(8,128)(2,1)S(1)}, u32[]{:S(2)}, u32[]{:S(2)}) %collective-permute-start.8) | collective-permute-done | bytes 73760 | tf_op jit(solution)/shard_map/ppermute | solution.py:262
  30.5 0.0 collective-permute-done.7
  30.5 0.8 %level1.1 = (f32[8,1024]{1,0:T(8,128)}, f32[32,1152]{1,0:T(8,128)S(1)}) custom-call(f32[32,1152]{1,0:T(8,128)S(1)} %partial_sums.1.refs_0_, f32[32,1152]{1,0:T(8,128)S(1)} %convert_element_type.22.refs_1_, f32[32,1152]{1,0:T(8,128)S(1)} %convert_element_type.23.refs_2_, f32[32,1152]{1,0:T(8,128)S(1)} %convert_element_type.24.refs_3_, ...), custom_call_target="tpu_custom_call" | custom-call | tf_op jit(solution)/shard_map/level1/pallas_call | solution.py:318
  31.3 1.1 %collective-permute-start.12 = (f16[32,1152]{1,0:T(8,128)(2,1)S(1)}, f16[32,1152]{1,0:T(8,128)(2,1)S(1)}, u32[]{:S(2)}, u32[]{:S(2)}) collective-permute-start(f16[32,1152]{1,0:T(8,128)(2,1)S(1)} %convert_element_type.25), channel_id=1, source_target_pairs={{0,6},{1,7},{2,4},{3,5},{4,2},{5,3},{6,0},{7,1},{8,14},{9,15},{10,... | collective-permute-start | bytes 221192 | tf_op jit(solution)/shard_map/ppermute | solution.py:262
  32.5 0.9 %collective-permute-start.11 = (f16[32,1152]{1,0:T(8,128)(2,1)S(1)}, f16[32,1152]{1,0:T(8,128)(2,1)S(1)}, u32[]{:S(2)}, u32[]{:S(2)}) collective-permute-start(f16[32,1152]{1,0:T(8,128)(2,1)S(1)} %convert_element_type.25), channel_id=1, source_target_pairs={{0,4},{1,5},{2,6},{3,7},{4,0},{5,1},{6,2},{7,3},{8,12},{9,13},{10,... | collective-permute-start | bytes 221192 | tf_op jit(solution)/shard_map/ppermute | solution.py:262
  33.3 1.6 %collective-permute-start.10 = (f16[32,1152]{1,0:T(8,128)(2,1)S(1)}, f16[32,1152]{1,0:T(8,128)(2,1)S(1)}, u32[]{:S(2)}, u32[]{:S(2)}) collective-permute-start(f16[32,1152]{1,0:T(8,128)(2,1)S(1)} %convert_element_type.25), channel_id=1, source_target_pairs={{0,2},{1,3},{2,0},{3,1},{4,6},{5,7},{6,4},{7,5},{8,10},{9,11},{10,... | collective-permute-start | bytes 221192 | tf_op jit(solution)/shard_map/ppermute | solution.py:262
  34.9 2.3 %collective-permute-done.12 = f16[32,1152]{1,0:T(8,128)(2,1)S(1)} collective-permute-done((f16[32,1152]{1,0:T(8,128)(2,1)S(1)}, f16[32,1152]{1,0:T(8,128)(2,1)S(1)}, u32[]{:S(2)}, u32[]{:S(2)}) %collective-permute-start.12) | collective-permute-done | bytes 73760 | tf_op jit(solution)/shard_map/ppermute | solution.py:262
  37.2 0.0 collective-permute-start.16
  37.2 0.4 collective-permute-done.11
  37.5 0.1 collective-permute-start.15
  37.7 0.0 collective-permute-done.10
  37.7 0.4 collective-permute-start.14
  38.1 0.9 %maximum_convert_fusion.refs_0_ = f32[128,1152]{1,0:T(8,128)} fusion(f16[32,1152]{1,0:T(8,128)(2,1)S(1)} %collective-permute-done.12, f16[32,1152]{1,0:T(8,128)(2,1)S(1)} %collective-permute-done.11, f16[32,1152]{1,0:T(8,128)(2,1)S(1)} %collective-permute-done.10, f16[32,1152]{1,0:T(8,128)(2,1)S(1)} %convert_element_type.25), kind=kLoop, calls=%fused_computation | loop fusion | flops 589824 | bytes 884736 | tf_op jit(solution)/shard_map/convert_element_type | solution.py:354
  39.0 0.0 collective-permute-done.14
  39.0 0.9 %maximum_convert_fusion.1.refs_1_ = f32[128,1152]{1,0:T(8,128)} fusion(f16[32,1152]{1,0:T(8,128)(2,1)S(1)} %collective-permute-done.16, f16[32,1152]{1,0:T(8,128)(2,1)S(1)} %collective-permute-done.15, f16[32,1152]{1,0:T(8,128)(2,1)S(1)} %collective-permute-done.14, f16[32,1152]{1,0:T(8,128)(2,1)S(1)} %collective-permute-done.13), kind=kLoop, calls=%fused_computation.1 | loop fusion | flops 589824 | bytes 884736 | tf_op jit(solution)/shard_map/convert_element_type | solution.py:354
  39.9 8.1 %scores.1 = (f32[64,128]{1,0:T(8,128)}, f32[32,1024]{1,0:T(8,128)}, f32[256,1024]{1,0:T(8,128)}) custom-call(s32[64]{0:T(128)} %rows_ref.1, bf16[8192,1024]{1,0:T(8,128)(2,1)S(1)} %get-tuple-element.29.live_ref, f32[128,1152]{1,0:T(8,128)} %maximum_convert_fusion.refs_0_, f32[128,1152]{1,0:T(8,128)} %maximum_convert_fusion.1.refs_1_), custom_call_target="tpu_custom_call" | custom-call | tf_op jit(solution)/shard_map/scores/pallas_call | solution.py:333
  (13 shorter events, 0.1 us)
Async XLA Ops:
  7.9 5.0 %collective-permute-start = (f32[8,1152]{1,0:T(8,128)S(1)}, f32[8,1152]{1,0:T(8,128)S(1)}, u32[]{:S(2)}, u32[]{:S(2)}) collective-permute-start(f32[8,1152]{1,0:T(8,128)S(1)} %get-tuple-element.20), channel_id=1, source_target_pairs={{0,1},{1,0},{2,3},{3,2},{4,5},{5,4},{6,7},{7,6},{8,9},{9,8},{10,11... | collective-permute-start | bytes 110600 | tf_op jit(solution)/shard_map/ppermute | solution.py:262
  8.4 7.0 %collective-permute-start.1 = (f32[8,1152]{1,0:T(8,128)S(1)}, f32[8,1152]{1,0:T(8,128)S(1)}, u32[]{:S(2)}, u32[]{:S(2)}) collective-permute-start(f32[8,1152]{1,0:T(8,128)S(1)} %get-tuple-element.21), channel_id=1, source_target_pairs={{0,2},{1,3},{2,0},{3,1},{4,6},{5,7},{6,4},{7,5},{8,10},{9,11},{10,... | collective-permute-start | bytes 110600 | tf_op jit(solution)/shard_map/ppermute | solution.py:262
  10.9 4.7 %collective-permute-start.2 = (f32[8,1152]{1,0:T(8,128)S(1)}, f32[8,1152]{1,0:T(8,128)S(1)}, u32[]{:S(2)}, u32[]{:S(2)}) collective-permute-start(f32[8,1152]{1,0:T(8,128)S(1)} %get-tuple-element.22), channel_id=1, source_target_pairs={{0,3},{1,2},{2,1},{3,0},{4,7},{5,6},{6,5},{7,4},{8,11},{9,10},{10,... | collective-permute-start | bytes 110600 | tf_op jit(solution)/shard_map/ppermute | solution.py:262
  11.0 4.7 %collective-permute-start.3 = (f32[8,1152]{1,0:T(8,128)S(1)}, f32[8,1152]{1,0:T(8,128)S(1)}, u32[]{:S(2)}, u32[]{:S(2)}) collective-permute-start(f32[8,1152]{1,0:T(8,128)S(1)} %get-tuple-element.23), channel_id=1, source_target_pairs={{0,4},{1,5},{2,6},{3,7},{4,0},{5,1},{6,2},{7,3},{8,12},{9,13},{10,... | collective-permute-start | bytes 110600 | tf_op jit(solution)/shard_map/ppermute | solution.py:262
  12.9 3.5 %collective-permute-start.4 = (f32[8,1152]{1,0:T(8,128)S(1)}, f32[8,1152]{1,0:T(8,128)S(1)}, u32[]{:S(2)}, u32[]{:S(2)}) collective-permute-start(f32[8,1152]{1,0:T(8,128)S(1)} %get-tuple-element.24), channel_id=1, source_target_pairs={{0,5},{1,4},{2,7},{3,6},{4,1},{5,0},{6,3},{7,2},{8,13},{9,12},{10,... | collective-permute-start | bytes 110600 | tf_op jit(solution)/shard_map/ppermute | solution.py:262
  12.9 4.9 %collective-permute-start.5 = (f32[8,1152]{1,0:T(8,128)S(1)}, f32[8,1152]{1,0:T(8,128)S(1)}, u32[]{:S(2)}, u32[]{:S(2)}) collective-permute-start(f32[8,1152]{1,0:T(8,128)S(1)} %get-tuple-element.25), channel_id=1, source_target_pairs={{0,6},{1,7},{2,4},{3,5},{4,2},{5,3},{6,0},{7,1},{8,14},{9,15},{10,... | collective-permute-start | bytes 110600 | tf_op jit(solution)/shard_map/ppermute | solution.py:262
  15.5 4.3 %collective-permute-start.6 = (f32[8,1152]{1,0:T(8,128)S(1)}, f32[8,1152]{1,0:T(8,128)S(1)}, u32[]{:S(2)}, u32[]{:S(2)}) collective-permute-start(f32[8,1152]{1,0:T(8,128)S(1)} %get-tuple-element.26), channel_id=1, source_target_pairs={{0,7},{1,6},{2,5},{3,4},{4,3},{5,2},{6,1},{7,0},{8,15},{9,14},{10,... | collective-permute-start | bytes 110600 | tf_op jit(solution)/shard_map/ppermute | solution.py:262
  20.2 6.8 %collective-permute-start.9 = (f16[32,1152]{1,0:T(8,128)(2,1)S(1)}, f16[32,1152]{1,0:T(8,128)(2,1)S(1)}, u32[]{:S(2)}, u32[]{:S(2)}) collective-permute-start(f16[32,1152]{1,0:T(8,128)(2,1)S(1)} %convert_element_type.21), channel_id=1, source_target_pairs={{0,24},{1,25},{2,26},{3,27},{4,28},{5,29},{6,30},{7,31},{8,16},{9,... | collective-permute-start | bytes 221192 | tf_op jit(solution)/shard_map/ppermute | solution.py:262
  24.1 6.4 %collective-permute-start.8 = (f16[32,1152]{1,0:T(8,128)(2,1)S(1)}, f16[32,1152]{1,0:T(8,128)(2,1)S(1)}, u32[]{:S(2)}, u32[]{:S(2)}) collective-permute-start(f16[32,1152]{1,0:T(8,128)(2,1)S(1)} %convert_element_type.21), channel_id=1, source_target_pairs={{0,16},{1,17},{2,18},{3,19},{4,20},{5,21},{6,22},{7,23},{8,24},{9,... | collective-permute-start | bytes 221192 | tf_op jit(solution)/shard_map/ppermute | solution.py:262
  24.1 6.4 %collective-permute-start.7 = (f16[32,1152]{1,0:T(8,128)(2,1)S(1)}, f16[32,1152]{1,0:T(8,128)(2,1)S(1)}, u32[]{:S(2)}, u32[]{:S(2)}) collective-permute-start(f16[32,1152]{1,0:T(8,128)(2,1)S(1)} %convert_element_type.21), channel_id=1, source_target_pairs={{0,8},{1,9},{2,10},{3,11},{4,12},{5,13},{6,14},{7,15},{8,0},{9,1},... | collective-permute-start | bytes 221192 | tf_op jit(solution)/shard_map/ppermute | solution.py:262
  31.3 5.8 %collective-permute-start.12 = (f16[32,1152]{1,0:T(8,128)(2,1)S(1)}, f16[32,1152]{1,0:T(8,128)(2,1)S(1)}, u32[]{:S(2)}, u32[]{:S(2)}) collective-permute-start(f16[32,1152]{1,0:T(8,128)(2,1)S(1)} %convert_element_type.25), channel_id=1, source_target_pairs={{0,6},{1,7},{2,4},{3,5},{4,2},{5,3},{6,0},{7,1},{8,14},{9,15},{10,... | collective-permute-start | bytes 221192 | tf_op jit(solution)/shard_map/ppermute | solution.py:262
  32.5 5.1 %collective-permute-start.11 = (f16[32,1152]{1,0:T(8,128)(2,1)S(1)}, f16[32,1152]{1,0:T(8,128)(2,1)S(1)}, u32[]{:S(2)}, u32[]{:S(2)}) collective-permute-start(f16[32,1152]{1,0:T(8,128)(2,1)S(1)} %convert_element_type.25), channel_id=1, source_target_pairs={{0,4},{1,5},{2,6},{3,7},{4,0},{5,1},{6,2},{7,3},{8,12},{9,13},{10,... | collective-permute-start | bytes 221192 | tf_op jit(solution)/shard_map/ppermute | solution.py:262
  33.3 4.4 %collective-permute-start.10 = (f16[32,1152]{1,0:T(8,128)(2,1)S(1)}, f16[32,1152]{1,0:T(8,128)(2,1)S(1)}, u32[]{:S(2)}, u32[]{:S(2)}) collective-permute-start(f16[32,1152]{1,0:T(8,128)(2,1)S(1)} %convert_element_type.25), channel_id=1, source_target_pairs={{0,2},{1,3},{2,0},{3,1},{4,6},{5,7},{6,4},{7,5},{8,10},{9,11},{10,... | collective-permute-start | bytes 221192 | tf_op jit(solution)/shard_map/ppermute | solution.py:262
  34.9 4.1 %collective-permute-start.13 = (f16[32,1152]{1,0:T(8,128)(2,1)S(1)}, f16[32,1152]{1,0:T(8,128)(2,1)S(1)}, u32[]{:S(2)}, u32[]{:S(2)}) collective-permute-start(f16[32,1152]{1,0:T(8,128)(2,1)S(1)} %convert_element_type.25), channel_id=1, source_target_pairs={{0,1},{1,0},{2,3},{3,2},{4,5},{5,4},{6,7},{7,6},{8,9},{9,8},{10,11... | collective-permute-start | bytes 221192 | tf_op jit(solution)/shard_map/ppermute | solution.py:262
  37.2 1.8 %collective-permute-start.16 = (f16[32,1152]{1,0:T(8,128)(2,1)S(1)}, f16[32,1152]{1,0:T(8,128)(2,1)S(1)}, u32[]{:S(2)}, u32[]{:S(2)}) collective-permute-start(f16[32,1152]{1,0:T(8,128)(2,1)S(1)} %collective-permute-done.12), channel_id=1, source_target_pairs={{0,1},{1,0},{2,3},{3,2},{4,5},{5,4},{6,7},{7,6},{8,9},{9,8},{10,11... | collective-permute-start | bytes 221192 | tf_op jit(solution)/shard_map/ppermute | solution.py:262
  37.5 1.4 %collective-permute-start.15 = (f16[32,1152]{1,0:T(8,128)(2,1)S(1)}, f16[32,1152]{1,0:T(8,128)(2,1)S(1)}, u32[]{:S(2)}, u32[]{:S(2)}) collective-permute-start(f16[32,1152]{1,0:T(8,128)(2,1)S(1)} %collective-permute-done.11), channel_id=1, source_target_pairs={{0,1},{1,0},{2,3},{3,2},{4,5},{5,4},{6,7},{7,6},{8,9},{9,8},{10,11... | collective-permute-start | bytes 221192 | tf_op jit(solution)/shard_map/ppermute | solution.py:262
  37.7 1.3 %collective-permute-start.14 = (f16[32,1152]{1,0:T(8,128)(2,1)S(1)}, f16[32,1152]{1,0:T(8,128)(2,1)S(1)}, u32[]{:S(2)}, u32[]{:S(2)}) collective-permute-start(f16[32,1152]{1,0:T(8,128)(2,1)S(1)} %collective-permute-done.10), channel_id=1, source_target_pairs={{0,1},{1,0},{2,3},{3,2},{4,5},{5,4},{6,7},{7,6},{8,9},{9,8},{10,11... | collective-permute-start | bytes 221192 | tf_op jit(solution)/shard_map/ppermute | solution.py:262
